TPU v7x, 256 devices: a whole 4x4x8 slice. The times are simulated.
256 devices in a mesh: south: 2 (over z_2), east: 4 (over z_1, core), down: 8 (over z_0, x), ens: 4 (over y).
Axes of the slice: x: 4, y: 4, z: 8 (z_0: 2, z_1: 2, z_2: 2; z = z_0 * 4 + z_1 * 2 + z_2), core: 2. Of those that a mesh axis runs over, the one named last changes fastest.
Arguments:
- density: float32 [32, 128, 512, 128], P(('ens', 'south'), 'east', 'down'), parts along dimension 0, may hold values from 0.2 to 1.8
- flow_j: float32 [32, 128, 512, 128], P(('ens', 'south'), 'east', 'down'), parts along dimension 0, may hold values from -0.3 to 0.3
- flow_i: float32 [32, 128, 512, 128], P(('ens', 'south'), 'east', 'down'), parts along dimension 0, may hold values from -0.3 to 0.3
- flow_k: float32 [32, 128, 512, 128], P(('ens', 'south'), 'east', 'down'), parts along dimension 0, may hold values from -0.3 to 0.3
Outputs:
- density_end: float32 [32, 128, 512, 128], P(('ens', 'south'), 'east', 'down'), parts along dimension 0
There are 4 independent parts, one for each index of `ens`. A program takes and returns all parts, laid end to end along the dimension named above; each array names one. Nothing has to cross between parts.
All inputs are finite; a program needn't handle non-finite values.
Results may differ from a plain program's by a relative error of at most 0.00002.
Values sent between devices are 32-bit elements; how exact they have to be, the bound alone decides.
A program may use at most 192 MiB of HBM per device.

v0:
```python
import jax
import jax.numpy as jnp
from jax import lax
from jax.sharding import PartitionSpec as P

STEPS = 3


def extended(x, sides, width):
    edges = {}
    for axis, dim in sides:
        count, length = (lax.axis_size(axis), x.shape[dim])
        up = [(i, (i + 1) % count) for i in range(count - 1)]
        last = lax.slice_in_dim(x, length - width, length, axis=dim)
        initial = lax.slice_in_dim(x, 0, width, axis=dim)
        edges[dim] = (
            lax.ppermute(last, axis, up),
            lax.ppermute(initial, axis, [(b, a) for a, b in up]),
        )
    done = []
    for _, dim in sides:
        low, high = edges[dim]
        around = [(width, width) if d in done else (0, 0) for d in range(x.ndim)]
        x = jnp.concatenate([jnp.pad(low, around), x, jnp.pad(high, around)], axis=dim)
        done.append(dim)
    return x


def inner_cells(values, dims):
    for dim in dims:
        values = lax.slice_in_dim(values, 1, values.shape[dim] - 1, axis=dim)
    return values


def side_cells(values, dim, start, dims):
    others = [other for other in dims if other != dim]
    values = inner_cells(values, others)
    return lax.slice_in_dim(values, start, start + values.shape[dim] - 2, axis=dim)


def advance(padded, flow_j, flow_i, flow_k):
    middle = inner_cells(padded, (0, 1, 2))
    lower = [side_cells(padded, dim, 0, (0, 1, 2)) for dim in (0, 1, 2)]
    upper = [side_cells(padded, dim, 2, (0, 1, 2)) for dim in (0, 1, 2)]
    slopes = [above - below for above, below in zip(upper, lower)]
    smooth_rate = 0.05
    spread = lower[0] + upper[0] + lower[1] + upper[1] + lower[2] + upper[2] - 6.0 * middle
    return (
        middle - flow_j * slopes[0] - flow_i * slopes[1] - flow_k * slopes[2] + smooth_rate * spread
    )


def per_device(density, flow_j, flow_i, flow_k):
    for step in range(STEPS):
        padded = extended(density, (("south", 0), ("east", 1), ("down", 2)), 1)
        density = advance(padded, flow_j, flow_i, flow_k)
    return density


def solution(mesh):
    in_specs = (
        P(("ens", "south"), "east", "down", None),
        P(("ens", "south"), "east", "down", None),
        P(("ens", "south"), "east", "down", None),
        P(("ens", "south"), "east", "down", None),
    )
    out_specs = P(("ens", "south"), "east", "down", None)
    return jax.shard_map(
        per_device, mesh=mesh, in_specs=in_specs, out_specs=out_specs, check_vma=False
    )
```

profile of v0, /device:TPU:7, one launch (start us, length us, event | category | flops | bytes accessed | tf_op | source)
XLA Modules:
  0.0 154.5 jit_solution(14344505556304568645)
XLA Ops:
  0.0 1.8 %fusion.14 = (f32[1,32,64,128]{3,2,1,0:T(8,128)S(1)}, f32[1,32,64,128]{3,2,1,0:T(8,128)S(1)}) fusion(f32[4,32,64,128]{3,2,1,0:T(8,128)} %param.4), kind=kLoop, calls=%fused_computation.68 | loop fusion | bytes 4194304 | tf_op jit(solution)/shard_map/slice | solution.py:15
  1.8 3.7 %collective-permute-start.1 = (f32[1,32,64,128]{3,2,1,0:T(8,128)S(1)}, f32[1,32,64,128]{3,2,1,0:T(8,128)S(1)}, u32[]{:S(2)}, u32[]{:S(2)}) collective-permute-start(f32[1,32,64,128]{3,2,1,0:T(8,128)S(1)} %get-tuple-element.22), channel_id=1, source_target_pairs={{0,128},{1,129},{2,130},{3,131},{4,132},{5,133},{6,134},{7,135},{8... | collective-permute-start | bytes 3145736 | tf_op jit(solution)/shard_map/ppermute | solution.py:17
  5.6 1.3 collective-permute-start
  6.9 2.9 %collective-permute-start.2 = (f32[4,1,64,128]{3,2,1,0:T(8,128)S(1)}, f32[4,1,64,128]{3,2,1,0:T(8,128)S(1)}, u32[]{:S(2)}, u32[]{:S(2)}) collective-permute-start(f32[4,1,64,128]{3,2,1,0:T(8,128)S(1)} %get-tuple-element.20), channel_id=1, source_target_pairs={{32,0},{64,32},{96,64},{33,1},{65,33},{97,65},{34,2},{66,34},{98,6... | collective-permute-start | bytes 393224 | tf_op jit(solution)/shard_map/ppermute | solution.py:18
  9.8 4.8 %collective-permute-start.3 = (f32[4,1,64,128]{3,2,1,0:T(8,128)S(1)}, f32[4,1,64,128]{3,2,1,0:T(8,128)S(1)}, u32[]{:S(2)}, u32[]{:S(2)}) collective-permute-start(f32[4,1,64,128]{3,2,1,0:T(8,128)S(1)} %get-tuple-element.19), channel_id=1, source_target_pairs={{0,32},{32,64},{64,96},{1,33},{33,65},{65,97},{2,34},{34,66},{66,9... | collective-permute-start | bytes 393224 | tf_op jit(solution)/shard_map/ppermute | solution.py:17
  14.6 0.1 fusion.12
  14.7 2.5 %collective-permute-start.4 = (f32[4,32,1,128]{3,2,1,0:T(1,128)S(1)}, f32[4,32,1,128]{3,2,1,0:T(1,128)}, u32[]{:S(2)}, u32[]{:S(2)}) collective-permute-start(f32[4,32,1,128]{3,2,1,0:T(1,128)S(1)} %get-tuple-element.18), channel_id=1, source_target_pairs={{4,0},{8,4},{12,8},{16,12},{20,16},{24,20},{28,24},{5,1},{9,5},{13... | collective-permute-start | bytes 196616 | tf_op jit(solution)/shard_map/ppermute | solution.py:18
  17.2 0.0 collective-permute-done.2
  17.2 8.8 %collective-permute-start.5 = (f32[4,32,1,128]{3,2,1,0:T(1,128)S(1)}, f32[4,32,1,128]{3,2,1,0:T(1,128)}, u32[]{:S(2)}, u32[]{:S(2)}) collective-permute-start(f32[4,32,1,128]{3,2,1,0:T(1,128)S(1)} %get-tuple-element.17), channel_id=1, source_target_pairs={{0,4},{4,8},{8,12},{12,16},{16,20},{20,24},{24,28},{1,5},{5,9},{9,... | collective-permute-start | bytes 196616 | tf_op jit(solution)/shard_map/ppermute | solution.py:17
  26.1 4.1 %collective-permute-done.3 = f32[4,1,64,128]{3,2,1,0:T(8,128)S(1)} collective-permute-done((f32[4,1,64,128]{3,2,1,0:T(8,128)S(1)}, f32[4,1,64,128]{3,2,1,0:T(8,128)S(1)}, u32[]{:S(2)}, u32[]{:S(2)}) %collective-permute-start.3) | collective-permute-done | bytes 131104 | tf_op jit(solution)/shard_map/ppermute | solution.py:17
  30.2 0.0 collective-permute-done.1
  30.2 1.1 constant_dynamic-update-slice_fusion.2
  31.2 2.4 %constant_dynamic-update-slice_fusion.1 = f32[6,32,64,128]{3,2,1,0:T(8,128)} fusion(f32[6,32,64,128]{3,2,1,0:T(8,128)} %constant_dynamic-update-slice_fusion.2, f32[4,32,64,128]{3,2,1,0:T(8,128)S(1)} %copy-done.3), kind=kLoop, calls=%fused_computation.58 | loop fusion | bytes 8388608
  33.7 0.0 collective-permute-done
  33.7 1.1 constant_dynamic-update-slice_fusion
  34.7 3.1 %collective-permute-done.4 = f32[4,32,1,128]{3,2,1,0:T(1,128)} collective-permute-done((f32[4,32,1,128]{3,2,1,0:T(1,128)S(1)}, f32[4,32,1,128]{3,2,1,0:T(1,128)}, u32[]{:S(2)}, u32[]{:S(2)}) %collective-permute-start.4) | collective-permute-done | bytes 65568 | tf_op jit(solution)/shard_map/ppermute | solution.py:18
  37.9 0.0 collective-permute-done.5
  37.9 15.1 %multiply_add_fusion.2 = f32[4,32,64,128]{3,2,1,0:T(8,128)} fusion(f32[4,32,64,128]{3,2,1,0:T(8,128)} %param.4, f32[4,32,64,128]{3,2,1,0:T(8,128)S(1)} %copy-done, f32[4,32,1,128]{3,2,1,0:T(1,128)} %collective-permute-done.4, f32[6,1,64,128]{3,2,1,0:T(8,128)S(1)} %pad.38, f32[6,32,64,128]{3,2,1,0:T(8,128)} %constant_dynamic-update-slice_fusion, ...), kind=kLoop, calls=%fused_computation.56 | loop fusion | flops 35651584 | bytes 29884416 | tf_op jit(solution)/shard_map/add | solution.py:49
  53.0 1.9 %fusion.11 = (f32[1,32,64,128]{3,2,1,0:T(8,128)S(1)}, f32[1,32,64,128]{3,2,1,0:T(8,128)S(1)}) fusion(f32[4,32,64,128]{3,2,1,0:T(8,128)} %multiply_add_fusion.2), kind=kLoop, calls=%fused_computation.65 | loop fusion | bytes 4194304 | tf_op jit(solution)/shard_map/slice | solution.py:14
  54.9 1.3 collective-permute-start.6
  56.2 13.3 %collective-permute-start.7 = (f32[1,32,64,128]{3,2,1,0:T(8,128)S(1)}, f32[1,32,64,128]{3,2,1,0:T(8,128)S(1)}, u32[]{:S(2)}, u32[]{:S(2)}) collective-permute-start(f32[1,32,64,128]{3,2,1,0:T(8,128)S(1)} %get-tuple-element.15), channel_id=1, source_target_pairs={{0,128},{1,129},{2,130},{3,131},{4,132},{5,133},{6,134},{7,135},{8... | collective-permute-start | bytes 3145736 | tf_op jit(solution)/shard_map/ppermute | solution.py:17
  69.5 1.0 fusion.10
  70.5 1.9 %collective-permute-start.8 = (f32[4,1,64,128]{3,2,1,0:T(8,128)S(1)}, f32[4,1,64,128]{3,2,1,0:T(8,128)S(1)}, u32[]{:S(2)}, u32[]{:S(2)}) collective-permute-start(f32[4,1,64,128]{3,2,1,0:T(8,128)S(1)} %get-tuple-element.14), channel_id=1, source_target_pairs={{32,0},{64,32},{96,64},{33,1},{65,33},{97,65},{34,2},{66,34},{98,6... | collective-permute-start | bytes 393224 | tf_op jit(solution)/shard_map/ppermute | solution.py:18
  72.4 4.5 %collective-permute-start.9 = (f32[4,1,64,128]{3,2,1,0:T(8,128)S(1)}, f32[4,1,64,128]{3,2,1,0:T(8,128)S(1)}, u32[]{:S(2)}, u32[]{:S(2)}) collective-permute-start(f32[4,1,64,128]{3,2,1,0:T(8,128)S(1)} %get-tuple-element.13), channel_id=1, source_target_pairs={{0,32},{32,64},{64,96},{1,33},{33,65},{65,97},{2,34},{34,66},{66,9... | collective-permute-start | bytes 393224 | tf_op jit(solution)/shard_map/ppermute | solution.py:17
  77.0 1.3 fusion.9
  78.3 1.9 %collective-permute-start.10 = (f32[4,32,1,128]{3,2,1,0:T(1,128)S(1)}, f32[4,32,1,128]{3,2,1,0:T(1,128)S(1)}, u32[]{:S(2)}, u32[]{:S(2)}) collective-permute-start(f32[4,32,1,128]{3,2,1,0:T(1,128)S(1)} %get-tuple-element.12), channel_id=1, source_target_pairs={{4,0},{8,4},{12,8},{16,12},{20,16},{24,20},{28,24},{5,1},{9,5},{13... | collective-permute-start | bytes 196616 | tf_op jit(solution)/shard_map/ppermute | solution.py:18
  80.2 0.0 collective-permute-done.8
  80.2 9.4 %collective-permute-start.11 = (f32[4,32,1,128]{3,2,1,0:T(1,128)S(1)}, f32[4,32,1,128]{3,2,1,0:T(1,128)S(1)}, u32[]{:S(2)}, u32[]{:S(2)}) collective-permute-start(f32[4,32,1,128]{3,2,1,0:T(1,128)S(1)} %get-tuple-element.11), channel_id=1, source_target_pairs={{0,4},{4,8},{8,12},{12,16},{16,20},{20,24},{24,28},{1,5},{5,9},{9,... | collective-permute-start | bytes 196616 | tf_op jit(solution)/shard_map/ppermute | solution.py:17
  89.6 0.0 collective-permute-done.9
  89.7 2.6 %collective-permute-done.10 = f32[4,32,1,128]{3,2,1,0:T(1,128)S(1)} collective-permute-done((f32[4,32,1,128]{3,2,1,0:T(1,128)S(1)}, f32[4,32,1,128]{3,2,1,0:T(1,128)S(1)}, u32[]{:S(2)}, u32[]{:S(2)}) %collective-permute-start.10) | collective-permute-done | bytes 65568 | tf_op jit(solution)/shard_map/ppermute | solution.py:18
  92.2 0.0 collective-permute-done.11
  92.2 0.0 collective-permute-done.6
  92.3 14.1 %multiply_add_fusion.1 = f32[4,32,64,128]{3,2,1,0:T(8,128)S(1)} fusion(f32[4,32,64,128]{3,2,1,0:T(8,128)} %multiply_add_fusion.2, f32[4,32,64,128]{3,2,1,0:T(8,128)S(1)} %copy-done, f32[4,32,1,128]{3,2,1,0:T(1,128)S(1)} %collective-permute-done.10, f32[6,1,64,128]{3,2,1,0:T(8,128)S(1)} %pad.42, f32[1,32,64,128]{3,2,1,0:T(8,128)S(1)} %collective-permute-done.6, ...), kind=kLoop, calls=%fused_computation.55 | loop fusion | flops 44040192 | bytes 23592960 | tf_op jit(solution)/shard_map/add | solution.py:49
  106.3 0.0 copy-start.2
  106.3 0.2 fusion.8
  106.6 1.6 %collective-permute-start.12 = (f32[1,32,64,128]{3,2,1,0:T(8,128)S(1)}, f32[1,32,64,128]{3,2,1,0:T(8,128)S(1)}, u32[]{:S(2)}, u32[]{:S(2)}) collective-permute-start(f32[1,32,64,128]{3,2,1,0:T(8,128)S(1)} %get-tuple-element.10), channel_id=1, source_target_pairs={{128,0},{129,1},{130,2},{131,3},{132,4},{133,5},{134,6},{135,7},{1... | collective-permute-start | bytes 3145736 | tf_op jit(solution)/shard_map/ppermute | solution.py:18
  108.1 4.1 %collective-permute-start.13 = (f32[1,32,64,128]{3,2,1,0:T(8,128)S(1)}, f32[1,32,64,128]{3,2,1,0:T(8,128)S(1)}, u32[]{:S(2)}, u32[]{:S(2)}) collective-permute-start(f32[1,32,64,128]{3,2,1,0:T(8,128)S(1)} %get-tuple-element.9), channel_id=1, source_target_pairs={{0,128},{1,129},{2,130},{3,131},{4,132},{5,133},{6,134},{7,135},{8... | collective-permute-start | bytes 3145736 | tf_op jit(solution)/shard_map/ppermute | solution.py:17
  112.3 1.9 %collective-permute-start.14 = (f32[4,1,64,128]{3,2,1,0:T(8,128)S(1)}, f32[4,1,64,128]{3,2,1,0:T(8,128)S(1)}, u32[]{:S(2)}, u32[]{:S(2)}) collective-permute-start(f32[4,1,64,128]{3,2,1,0:T(8,128)S(1)} %get-tuple-element.8), channel_id=1, source_target_pairs={{32,0},{64,32},{96,64},{33,1},{65,33},{97,65},{34,2},{66,34},{98,6... | collective-permute-start | bytes 393224 | tf_op jit(solution)/shard_map/ppermute | solution.py:18
  114.2 4.5 %collective-permute-start.15 = (f32[4,1,64,128]{3,2,1,0:T(8,128)S(1)}, f32[4,1,64,128]{3,2,1,0:T(8,128)S(1)}, u32[]{:S(2)}, u32[]{:S(2)}) collective-permute-start(f32[4,1,64,128]{3,2,1,0:T(8,128)S(1)} %get-tuple-element.7), channel_id=1, source_target_pairs={{0,32},{32,64},{64,96},{1,33},{33,65},{65,97},{2,34},{34,66},{66,9... | collective-permute-start | bytes 393224 | tf_op jit(solution)/shard_map/ppermute | solution.py:17
  118.8 0.1 fusion.6
  118.9 1.9 %collective-permute-start.16 = (f32[4,32,1,128]{3,2,1,0:T(1,128)S(1)}, f32[4,32,1,128]{3,2,1,0:T(1,128)S(1)}, u32[]{:S(2)}, u32[]{:S(2)}) collective-permute-start(f32[4,32,1,128]{3,2,1,0:T(1,128)S(1)} %get-tuple-element.6), channel_id=1, source_target_pairs={{4,0},{8,4},{12,8},{16,12},{20,16},{24,20},{28,24},{5,1},{9,5},{13... | collective-permute-start | bytes 196616 | tf_op jit(solution)/shard_map/ppermute | solution.py:18
  120.8 9.4 %collective-permute-start.17 = (f32[4,32,1,128]{3,2,1,0:T(1,128)S(1)}, f32[4,32,1,128]{3,2,1,0:T(1,128)S(1)}, u32[]{:S(2)}, u32[]{:S(2)}) collective-permute-start(f32[4,32,1,128]{3,2,1,0:T(1,128)S(1)} %get-tuple-element.5), channel_id=1, source_target_pairs={{0,4},{4,8},{8,12},{12,16},{16,20},{20,24},{24,28},{1,5},{5,9},{9,... | collective-permute-start | bytes 196616 | tf_op jit(solution)/shard_map/ppermute | solution.py:17
  130.2 5.5 %collective-permute-done.15 = f32[4,1,64,128]{3,2,1,0:T(8,128)S(1)} collective-permute-done((f32[4,1,64,128]{3,2,1,0:T(8,128)S(1)}, f32[4,1,64,128]{3,2,1,0:T(8,128)S(1)}, u32[]{:S(2)}, u32[]{:S(2)}) %collective-permute-start.15) | collective-permute-done | bytes 131104 | tf_op jit(solution)/shard_map/ppermute | solution.py:17
  135.7 9.2 %collective-permute-done.16 = f32[4,32,1,128]{3,2,1,0:T(1,128)S(1)} collective-permute-done((f32[4,32,1,128]{3,2,1,0:T(1,128)S(1)}, f32[4,32,1,128]{3,2,1,0:T(1,128)S(1)}, u32[]{:S(2)}, u32[]{:S(2)}) %collective-permute-start.16) | collective-permute-done | bytes 65568 | tf_op jit(solution)/shard_map/ppermute | solution.py:18
  144.9 0.0 collective-permute-done.17
  144.9 0.0 collective-permute-done.12
  144.9 0.0 collective-permute-done.13
  144.9 9.5 %multiply_add_fusion = f32[4,32,64,128]{3,2,1,0:T(8,128)} fusion(f32[4,32,64,128]{3,2,1,0:T(8,128)S(1)} %multiply_add_fusion.1, f32[4,32,64,128]{3,2,1,0:T(8,128)S(1)} %copy-done, f32[4,32,1,128]{3,2,1,0:T(1,128)S(1)} %collective-permute-done.16, f32[6,1,64,128]{3,2,1,0:T(8,128)S(1)} %pad.46, f32[1,32,64,128]{3,2,1,0:T(8,128)S(1)} %collective-permute-done.12, ...), kind=kLoop, calls=%fused_computation.54 | loop fusion | flops 44040192 | bytes 23592960 | tf_op jit(solution)/shard_map/add | solution.py:49
  (17 shorter events, 0.1 us)
Async XLA Ops:
  0.0 6.9 %copy-start.3 = (f32[4,32,64,128]{3,2,1,0:T(8,128)S(1)}, f32[4,32,64,128]{3,2,1,0:T(8,128)}, u32[]{:S(2)}) copy-start(f32[4,32,64,128]{3,2,1,0:T(8,128)} %param.4) | copy-start | bytes 12582916
  1.8 28.3 %collective-permute-start.1 = (f32[1,32,64,128]{3,2,1,0:T(8,128)S(1)}, f32[1,32,64,128]{3,2,1,0:T(8,128)S(1)}, u32[]{:S(2)}, u32[]{:S(2)}) collective-permute-start(f32[1,32,64,128]{3,2,1,0:T(8,128)S(1)} %get-tuple-element.22), channel_id=1, source_target_pairs={{0,128},{1,129},{2,130},{3,131},{4,132},{5,133},{6,134},{7,135},{8... | collective-permute-start | bytes 3145736 | tf_op jit(solution)/shard_map/ppermute | solution.py:17
  5.6 28.1 %collective-permute-start = (f32[1,32,64,128]{3,2,1,0:T(8,128)S(1)}, f32[1,32,64,128]{3,2,1,0:T(8,128)S(1)}, u32[]{:S(2)}, u32[]{:S(2)}) collective-permute-start(f32[1,32,64,128]{3,2,1,0:T(8,128)S(1)} %get-tuple-element.21), channel_id=1, source_target_pairs={{128,0},{129,1},{130,2},{131,3},{132,4},{133,5},{134,6},{135,7},{1... | collective-permute-start | bytes 3145736 | tf_op jit(solution)/shard_map/ppermute | solution.py:18
  6.9 10.2 %collective-permute-start.2 = (f32[4,1,64,128]{3,2,1,0:T(8,128)S(1)}, f32[4,1,64,128]{3,2,1,0:T(8,128)S(1)}, u32[]{:S(2)}, u32[]{:S(2)}) collective-permute-start(f32[4,1,64,128]{3,2,1,0:T(8,128)S(1)} %get-tuple-element.20), channel_id=1, source_target_pairs={{32,0},{64,32},{96,64},{33,1},{65,33},{97,65},{34,2},{66,34},{98,6... | collective-permute-start | bytes 393224 | tf_op jit(solution)/shard_map/ppermute | solution.py:18
  9.8 20.4 %collective-permute-start.3 = (f32[4,1,64,128]{3,2,1,0:T(8,128)S(1)}, f32[4,1,64,128]{3,2,1,0:T(8,128)S(1)}, u32[]{:S(2)}, u32[]{:S(2)}) collective-permute-start(f32[4,1,64,128]{3,2,1,0:T(8,128)S(1)} %get-tuple-element.19), channel_id=1, source_target_pairs={{0,32},{32,64},{64,96},{1,33},{33,65},{65,97},{2,34},{34,66},{66,9... | collective-permute-start | bytes 393224 | tf_op jit(solution)/shard_map/ppermute | solution.py:17
  14.7 23.2 %collective-permute-start.4 = (f32[4,32,1,128]{3,2,1,0:T(1,128)S(1)}, f32[4,32,1,128]{3,2,1,0:T(1,128)}, u32[]{:S(2)}, u32[]{:S(2)}) collective-permute-start(f32[4,32,1,128]{3,2,1,0:T(1,128)S(1)} %get-tuple-element.18), channel_id=1, source_target_pairs={{4,0},{8,4},{12,8},{16,12},{20,16},{24,20},{28,24},{5,1},{9,5},{13... | collective-permute-start | bytes 196616 | tf_op jit(solution)/shard_map/ppermute | solution.py:18
  17.2 20.7 %collective-permute-start.5 = (f32[4,32,1,128]{3,2,1,0:T(1,128)S(1)}, f32[4,32,1,128]{3,2,1,0:T(1,128)}, u32[]{:S(2)}, u32[]{:S(2)}) collective-permute-start(f32[4,32,1,128]{3,2,1,0:T(1,128)S(1)} %get-tuple-element.17), channel_id=1, source_target_pairs={{0,4},{4,8},{8,12},{12,16},{16,20},{20,24},{24,28},{1,5},{5,9},{9,... | collective-permute-start | bytes 196616 | tf_op jit(solution)/shard_map/ppermute | solution.py:17
  31.2 6.6 %copy-start = (f32[4,32,64,128]{3,2,1,0:T(8,128)S(1)}, f32[4,32,64,128]{3,2,1,0:T(8,128)}, u32[]{:S(2)}) copy-start(f32[4,32,64,128]{3,2,1,0:T(8,128)} %param.7) | copy-start | bytes 12582916
  53.0 39.3 %copy-start.1 = (f32[4,32,64,128]{3,2,1,0:T(8,128)S(1)}, f32[4,32,64,128]{3,2,1,0:T(8,128)}, u32[]{:S(2)}) copy-start(f32[4,32,64,128]{3,2,1,0:T(8,128)} %param.6) | copy-start | bytes 12582916
  54.9 37.3 %collective-permute-start.6 = (f32[1,32,64,128]{3,2,1,0:T(8,128)S(1)}, f32[1,32,64,128]{3,2,1,0:T(8,128)S(1)}, u32[]{:S(2)}, u32[]{:S(2)}) collective-permute-start(f32[1,32,64,128]{3,2,1,0:T(8,128)S(1)} %get-tuple-element.16), channel_id=1, source_target_pairs={{128,0},{129,1},{130,2},{131,3},{132,4},{133,5},{134,6},{135,7},{1... | collective-permute-start | bytes 3145736 | tf_op jit(solution)/shard_map/ppermute | solution.py:18
  56.2 36.0 %collective-permute-start.7 = (f32[1,32,64,128]{3,2,1,0:T(8,128)S(1)}, f32[1,32,64,128]{3,2,1,0:T(8,128)S(1)}, u32[]{:S(2)}, u32[]{:S(2)}) collective-permute-start(f32[1,32,64,128]{3,2,1,0:T(8,128)S(1)} %get-tuple-element.15), channel_id=1, source_target_pairs={{0,128},{1,129},{2,130},{3,131},{4,132},{5,133},{6,134},{7,135},{8... | collective-permute-start | bytes 3145736 | tf_op jit(solution)/shard_map/ppermute | solution.py:17
  70.5 9.7 %collective-permute-start.8 = (f32[4,1,64,128]{3,2,1,0:T(8,128)S(1)}, f32[4,1,64,128]{3,2,1,0:T(8,128)S(1)}, u32[]{:S(2)}, u32[]{:S(2)}) collective-permute-start(f32[4,1,64,128]{3,2,1,0:T(8,128)S(1)} %get-tuple-element.14), channel_id=1, source_target_pairs={{32,0},{64,32},{96,64},{33,1},{65,33},{97,65},{34,2},{66,34},{98,6... | collective-permute-start | bytes 393224 | tf_op jit(solution)/shard_map/ppermute | solution.py:18
  72.4 17.2 %collective-permute-start.9 = (f32[4,1,64,128]{3,2,1,0:T(8,128)S(1)}, f32[4,1,64,128]{3,2,1,0:T(8,128)S(1)}, u32[]{:S(2)}, u32[]{:S(2)}) collective-permute-start(f32[4,1,64,128]{3,2,1,0:T(8,128)S(1)} %get-tuple-element.13), channel_id=1, source_target_pairs={{0,32},{32,64},{64,96},{1,33},{33,65},{65,97},{2,34},{34,66},{66,9... | collective-permute-start | bytes 393224 | tf_op jit(solution)/shard_map/ppermute | solution.py:17
  78.3 13.9 %collective-permute-start.10 = (f32[4,32,1,128]{3,2,1,0:T(1,128)S(1)}, f32[4,32,1,128]{3,2,1,0:T(1,128)S(1)}, u32[]{:S(2)}, u32[]{:S(2)}) collective-permute-start(f32[4,32,1,128]{3,2,1,0:T(1,128)S(1)} %get-tuple-element.12), channel_id=1, source_target_pairs={{4,0},{8,4},{12,8},{16,12},{20,16},{24,20},{28,24},{5,1},{9,5},{13... | collective-permute-start | bytes 196616 | tf_op jit(solution)/shard_map/ppermute | solution.py:18
  80.2 12.0 %collective-permute-start.11 = (f32[4,32,1,128]{3,2,1,0:T(1,128)S(1)}, f32[4,32,1,128]{3,2,1,0:T(1,128)S(1)}, u32[]{:S(2)}, u32[]{:S(2)}) collective-permute-start(f32[4,32,1,128]{3,2,1,0:T(1,128)S(1)} %get-tuple-element.11), channel_id=1, source_target_pairs={{0,4},{4,8},{8,12},{12,16},{16,20},{20,24},{24,28},{1,5},{5,9},{9,... | collective-permute-start | bytes 196616 | tf_op jit(solution)/shard_map/ppermute | solution.py:17
  106.3 38.6 %copy-start.2 = (f32[4,32,64,128]{3,2,1,0:T(8,128)S(1)}, f32[4,32,64,128]{3,2,1,0:T(8,128)}, u32[]{:S(2)}) copy-start(f32[4,32,64,128]{3,2,1,0:T(8,128)} %param.5) | copy-start | bytes 12582916
  106.6 38.3 %collective-permute-start.12 = (f32[1,32,64,128]{3,2,1,0:T(8,128)S(1)}, f32[1,32,64,128]{3,2,1,0:T(8,128)S(1)}, u32[]{:S(2)}, u32[]{:S(2)}) collective-permute-start(f32[1,32,64,128]{3,2,1,0:T(8,128)S(1)} %get-tuple-element.10), channel_id=1, source_target_pairs={{128,0},{129,1},{130,2},{131,3},{132,4},{133,5},{134,6},{135,7},{1... | collective-permute-start | bytes 3145736 | tf_op jit(solution)/shard_map/ppermute | solution.py:18
  108.1 36.8 %collective-permute-start.13 = (f32[1,32,64,128]{3,2,1,0:T(8,128)S(1)}, f32[1,32,64,128]{3,2,1,0:T(8,128)S(1)}, u32[]{:S(2)}, u32[]{:S(2)}) collective-permute-start(f32[1,32,64,128]{3,2,1,0:T(8,128)S(1)} %get-tuple-element.9), channel_id=1, source_target_pairs={{0,128},{1,129},{2,130},{3,131},{4,132},{5,133},{6,134},{7,135},{8... | collective-permute-start | bytes 3145736 | tf_op jit(solution)/shard_map/ppermute | solution.py:17
  112.3 8.5 %collective-permute-start.14 = (f32[4,1,64,128]{3,2,1,0:T(8,128)S(1)}, f32[4,1,64,128]{3,2,1,0:T(8,128)S(1)}, u32[]{:S(2)}, u32[]{:S(2)}) collective-permute-start(f32[4,1,64,128]{3,2,1,0:T(8,128)S(1)} %get-tuple-element.8), channel_id=1, source_target_pairs={{32,0},{64,32},{96,64},{33,1},{65,33},{97,65},{34,2},{66,34},{98,6... | collective-permute-start | bytes 393224 | tf_op jit(solution)/shard_map/ppermute | solution.py:18
  114.2 21.5 %collective-permute-start.15 = (f32[4,1,64,128]{3,2,1,0:T(8,128)S(1)}, f32[4,1,64,128]{3,2,1,0:T(8,128)S(1)}, u32[]{:S(2)}, u32[]{:S(2)}) collective-permute-start(f32[4,1,64,128]{3,2,1,0:T(8,128)S(1)} %get-tuple-element.7), channel_id=1, source_target_pairs={{0,32},{32,64},{64,96},{1,33},{33,65},{65,97},{2,34},{34,66},{66,9... | collective-permute-start | bytes 393224 | tf_op jit(solution)/shard_map/ppermute | solution.py:17
  118.9 26.0 %collective-permute-start.16 = (f32[4,32,1,128]{3,2,1,0:T(1,128)S(1)}, f32[4,32,1,128]{3,2,1,0:T(1,128)S(1)}, u32[]{:S(2)}, u32[]{:S(2)}) collective-permute-start(f32[4,32,1,128]{3,2,1,0:T(1,128)S(1)} %get-tuple-element.6), channel_id=1, source_target_pairs={{4,0},{8,4},{12,8},{16,12},{20,16},{24,20},{28,24},{5,1},{9,5},{13... | collective-permute-start | bytes 196616 | tf_op jit(solution)/shard_map/ppermute | solution.py:18
  120.8 24.1 %collective-permute-start.17 = (f32[4,32,1,128]{3,2,1,0:T(1,128)S(1)}, f32[4,32,1,128]{3,2,1,0:T(1,128)S(1)}, u32[]{:S(2)}, u32[]{:S(2)}) collective-permute-start(f32[4,32,1,128]{3,2,1,0:T(1,128)S(1)} %get-tuple-element.5), channel_id=1, source_target_pairs={{0,4},{4,8},{8,12},{12,16},{16,20},{20,24},{24,28},{1,5},{5,9},{9,... | collective-permute-start | bytes 196616 | tf_op jit(solution)/shard_map/ppermute | solution.py:17
where the time goes:
time: 155 us; the launch traced here: 154 us
  starting transfers between devices  79.7 us (51%)
  other arithmetic  38.7 us (25%)
  waiting for transfers between devices  24.5 us (16%)
  local copies, waits for them, and re-layouts  11.2 us (7%)
    ppermute x9, starting transfers between devices, extended(): lax.ppermute(last, axis, up)  62.6 us
    add x3, other arithmetic, advance(): middle - flow_j * slopes[0] - flow_i * slopes[1] - flow_k * slopes[2]  38.7 us
    ppermute x9, starting transfers between devices, extended(): lax.ppermute(initial, axis, [(b, a) for a, b in up])  17.1 us
    ppermute x9, waiting for transfers between devices, extended(): lax.ppermute(initial, axis, [(b, a) for a, b in up])  14.9 us
    ppermute x9, waiting for transfers between devices, extended(): lax.ppermute(last, axis, up)  9.6 us
    slice x8, local copies, waits for them, and re-layouts, extended(): last = lax.slice_in_dim(x, length - width, length, axis=dim)  4.69 us
    unnamed x10, local copies, waits for them, and re-layouts  3.52 us
  transfers between devices with their start and end apart: 18, of which 5 were waited for; matrix products, arithmetic and copies ran while one was open for 5% of the time, Pallas kernels for 0%

commit v1 on v0

v1 whole, which is shorter than its diff:
```python
import functools

import jax
import jax.numpy as jnp
from jax import lax
from jax.experimental import pallas as pl
from jax.experimental.pallas import tpu as pltpu
from jax.sharding import PartitionSpec as P

STEPS = 3
SMOOTH = 0.05
PAD = 8


def kernel(
    sizes, width, den, fj, fi, fk, out, field, flow, k_send, k_recv,
    load_sem, store_sem, south_send, south_recv, east_send, east_recv, down_send, down_recv,
):
    n_south, n_east, n_down = sizes
    nj, ni, nk, _ = den.shape
    chunks = ni // (2 * width)
    south, east, down = (lax.axis_index(a) for a in ("south", "east", "down"))
    has_west, has_east = east > 0, east < n_east - 1
    has_up, has_down = down > 0, down < n_down - 1
    inner_k = pl.ds(PAD, nk)

    def to(axis, index):
        return dict(device_id={axis: index}, device_id_type=pl.DeviceIdType.MESH)

    loads = [pltpu.make_async_copy(den, field.at[0, pl.ds(1, nj), pl.ds(1, ni), inner_k], load_sem.at[0])]
    for x, src in enumerate((fj, fi, fk)):
        loads.append(pltpu.make_async_copy(src, flow.at[x], load_sem.at[x + 1]))
    for copy in loads:
        copy.start()

    barrier = pltpu.get_barrier_semaphore()
    pl.semaphore_signal(barrier, inc=1, **to("south", 1 - south))

    @pl.when(has_west)
    def _():
        pl.semaphore_signal(barrier, inc=1, **to("east", east - 1))

    @pl.when(has_east)
    def _():
        pl.semaphore_signal(barrier, inc=1, **to("east", east + 1))

    @pl.when(has_up)
    def _():
        pl.semaphore_signal(barrier, inc=1, **to("down", down - 1))

    @pl.when(has_down)
    def _():
        pl.semaphore_signal(barrier, inc=1, **to("down", down + 1))

    outside_j = jnp.where(south == 0, 0, nj + 1)

    def clear(n, _):
        for t in range(STEPS):
            field[t, outside_j, n + 1, inner_k] = jnp.zeros((nk, 128), jnp.float32)
        return 0

    lax.fori_loop(0, ni, clear, 0)
    for edge, at in ((jnp.logical_not(has_west), 0), (jnp.logical_not(has_east), ni + 1)):
        @pl.when(edge)
        def _(at=at):
            for t in range(STEPS):
                for j in range(nj):
                    field[t, j + 1, at, inner_k] = jnp.zeros((nk, 128), jnp.float32)
    for edge, side in ((jnp.logical_not(has_up), 0), (jnp.logical_not(has_down), 1)):
        @pl.when(edge)
        def _(side=side):
            for t in range(STEPS):
                for c in range(chunks):
                    k_recv[t, side, c] = jnp.zeros(k_recv.shape[3:], jnp.float32)

    near = (has_west, has_east, has_up, has_down)
    pl.semaphore_wait(barrier, 1 + sum(jnp.where(h, 1, 0) for h in near))

    def row_of(c, seg):
        return c * width if seg == 0 else ni - width - c * width

    my_j = jnp.where(south == 0, nj - 1, 0)
    their_j = jnp.where(south == 0, 0, nj + 1)

    def south_copy(t, c, seg):
        r = row_of(c, seg)
        if isinstance(t, int) and t == 0:
            src = den.at[my_j, pl.ds(r, width)]
        else:
            src = field.at[t, my_j + 1, pl.ds(r + 1, width), inner_k]
        return pltpu.make_async_remote_copy(
            src_ref=src, dst_ref=field.at[t, their_j, pl.ds(r + 1, width), inner_k],
            send_sem=south_send.at[t, c, seg], recv_sem=south_recv.at[t, c, seg], **to("south", 1 - south))

    def east_copy(t, side):
        r, dst, other = (0, ni + 1, east - 1) if side == 0 else (ni - 1, 0, east + 1)
        if t == 0:
            src = den.at[:, r]
        else:
            src = field.at[t, pl.ds(1, nj), r + 1, inner_k]
        return pltpu.make_async_remote_copy(
            src_ref=src, dst_ref=field.at[t, pl.ds(1, nj), dst, inner_k],
            send_sem=east_send.at[t, side], recv_sem=east_recv.at[t, 1 - side], **to("east", other))

    def down_copy(t, c, side):
        other = down - 1 if side == 0 else down + 1
        return pltpu.make_async_remote_copy(
            src_ref=k_send.at[t, side, c], dst_ref=k_recv.at[t, 1 - side, c],
            send_sem=down_send.at[t, c, side], recv_sem=down_recv.at[t, c, 1 - side], **to("down", other))

    def each(cond_low, cond_high, fn):
        for side, cond in ((0, cond_low), (1, cond_high)):
            @pl.when(cond)
            def _(side=side):
                fn(side)

    def first(c, _):
        for seg in (0, 1):
            south_copy(0, c, seg).start()
        return 0

    lax.fori_loop(0, chunks, first, 0)
    each(has_west, has_east, lambda side: east_copy(0, side).start())

    def pack(t, c, seg, w):
        r = row_of(c, seg) + w
        for j in range(nj):
            at = (seg * width + w) * nj + j
            k_send[t, 0, c, pl.ds(at, 1)] = field[t, j + 1, r + 1, pl.ds(PAD, 1)]
            k_send[t, 1, c, pl.ds(at, 1)] = field[t, j + 1, r + 1, pl.ds(PAD + nk - 1, 1)]

    def unpack(t, c, seg, w):
        r = row_of(c, seg) + w
        for j in range(nj):
            at = (seg * width + w) * nj + j
            field[t, j + 1, r + 1, pl.ds(PAD - 1, 1)] = k_recv[t, 0, c, pl.ds(at, 1)]
            field[t, j + 1, r + 1, pl.ds(PAD + nk, 1)] = k_recv[t, 1, c, pl.ds(at, 1)]

    loads[0].wait()

    def first_pack(c, _):
        for seg in (0, 1):
            for w in range(width):
                pack(0, c, seg, w)
        return 0

    lax.fori_loop(0, chunks, first_pack, 0)
    for copy in loads[1:]:
        copy.wait()

    def first_down(c, _):
        each(has_up, has_down, lambda side: down_copy(0, c, side).start())
        return 0

    lax.fori_loop(0, chunks, first_down, 0)

    def advance(t, r):
        for b in range(nk // 8):
            at = pl.ds(PAD + 8 * b, 8)
            column = [field[t, j, r + 1, at] for j in range(nj + 2)]
            for j in range(nj):
                mid, j_low, j_high = column[j + 1], column[j], column[j + 2]
                i_low, i_high = field[t, j + 1, r, at], field[t, j + 1, r + 2, at]
                k_low = field[t, j + 1, r + 1, pl.ds(PAD + 8 * b - 1, 8)]
                k_high = field[t, j + 1, r + 1, pl.ds(PAD + 8 * b + 1, 8)]
                here = pl.ds(8 * b, 8)
                spread = j_low + j_high + i_low + i_high + k_low + k_high - 6.0 * mid
                value = (
                    mid - flow[0, j, r, here] * (j_high - j_low) - flow[1, j, r, here] * (i_high - i_low)
                    - flow[2, j, r, here] * (k_high - k_low) + SMOOTH * spread
                )
                field[t + 1, j + 1, r + 1, at] = value

    def store_copy(c, seg):
        r = row_of(c, seg)
        return pltpu.make_async_copy(
            field.at[STEPS, pl.ds(1, nj), pl.ds(r + 1, width), inner_k], out.at[:, pl.ds(r, width)],
            store_sem.at[c, seg])

    def send(t, c):
        for seg in (0, 1):
            south_copy(t, c, seg).start()
        each(has_up, has_down, lambda side: down_copy(t, c, side).start())

    def store(c):
        for seg in (0, 1):
            store_copy(c, seg).start()

    for t in range(STEPS):
        def chunk(c, _, t=t):
            for seg in (0, 1):
                south_copy(t, c, seg).wait_recv()
            each(has_up, has_down, lambda side: down_copy(t, c, 1 - side).wait_recv())

            @pl.when(c == 0)
            def _():
                each(has_west, has_east, lambda side: east_copy(t, 1 - side).wait_recv())

            for seg in (0, 1):
                for w in range(width):
                    unpack(t, c, seg, w)

            def rows(w, _):
                for seg in (0, 1):
                    advance(t, row_of(c, seg) + w)
                return 0

            lax.fori_loop(0, width, rows, 0)
            if t < STEPS - 1:
                for seg in (0, 1):
                    for w in range(width):
                        pack(t + 1, c, seg, w)

                @pl.when(c > 0)
                def _():
                    send(t + 1, c - 1)

                @pl.when(c == 1)
                def _():
                    each(has_west, has_east, lambda side: east_copy(t + 1, side).start())

                if t > 0:
                    @pl.when(c == 0)
                    def _():
                        send(t, chunks - 1)
            else:
                @pl.when(c == 0)
                def _():
                    send(t, chunks - 1)

                @pl.when(c > 0)
                def _():
                    store(c - 1)
            return 0

        lax.fori_loop(0, chunks, chunk, 0)
    store(chunks - 1)

    def finish(c, _):
        for seg in (0, 1):
            for t in range(STEPS):
                south_copy(t, c, seg).wait_send()
            store_copy(c, seg).wait()
        for t in range(STEPS):
            each(has_up, has_down, lambda side: down_copy(t, c, side).wait_send())
        return 0

    lax.fori_loop(0, chunks, finish, 0)
    for t in range(STEPS):
        each(has_west, has_east, lambda side: east_copy(t, side).wait_send())


def solution(mesh, width=2):
    sizes = tuple(mesh.shape[a] for a in ("south", "east", "down"))

    def per_device(density, flow_j, flow_i, flow_k):
        nj, ni, nk, ns = density.shape
        chunks = ni // (2 * width)
        dma = pltpu.SemaphoreType.DMA
        return pl.pallas_call(
            functools.partial(kernel, sizes, width),
            out_shape=jax.ShapeDtypeStruct(density.shape, density.dtype),
            in_specs=[pl.BlockSpec(memory_space=pl.ANY)] * 4,
            out_specs=pl.BlockSpec(memory_space=pl.ANY),
            scratch_shapes=[
                pltpu.VMEM((STEPS + 1, nj + 2, ni + 2, nk + 2 * PAD, ns), jnp.float32),
                pltpu.VMEM((3, nj, ni, nk, ns), jnp.float32),
                pltpu.VMEM((STEPS, 2, chunks, 2 * width * nj, ns), jnp.float32),
                pltpu.VMEM((STEPS, 2, chunks, 2 * width * nj, ns), jnp.float32),
                dma((4,)),
                dma((chunks, 2)),
                dma((STEPS, chunks, 2)),
                dma((STEPS, chunks, 2)),
                dma((STEPS, 2)),
                dma((STEPS, 2)),
                dma((STEPS, chunks, 2)),
                dma((STEPS, chunks, 2)),
            ],
            compiler_params=pltpu.CompilerParams(
                collective_id=0, has_side_effects=True, vmem_limit_bytes=60 * 1024 * 1024
            ),
            name="advect",
        )(density, flow_j, flow_i, flow_k)

    spec = P(("ens", "south"), "east", "down", None)
    return jax.shard_map(per_device, mesh=mesh, in_specs=(spec,) * 4, out_specs=spec, check_vma=False)
```

time: 155 us -> 102 us (0.66)
  the two profiles are of different devices: /device:TPU:7 before, /device:TPU:38 now
where the time goes in v1:
time: 102 us; the launch traced here: 101 us
  Pallas kernels  96.7 us (95%)
  local copies, waits for them, and re-layouts  4.79 us (5%)
    pallas_call x1, Pallas kernels, per_device(): pl.pallas_call(functools.partial(kernel, sizes, width), out_shape=jax.Sha...  96.7 us
    unnamed x1, local copies, waits for them, and re-layouts  4.79 us

profile of v1, /device:TPU:38, one launch (start us, length us, event | category | flops | bytes accessed | tf_op | source)
XLA Modules:
  0.0 101.5 jit_solution(4414266883440673984)
XLA Ops:
  0.0 96.7 %advect.1 = f32[4,32,64,128]{3,2,1,0:T(8,128)} custom-call(f32[4,32,64,128]{3,2,1,0:T(8,128)} %den.1, f32[4,32,64,128]{3,2,1,0:T(8,128)} %fj.1, f32[4,32,64,128]{3,2,1,0:T(8,128)} %fi.1, f32[4,32,64,128]{3,2,1,0:T(8,128)} %fk.1), custom_call_target="tpu_custom_call" | custom-call | tf_op jit(solution)/shard_map/advect/pallas_call | solution.py:260
  96.7 4.8 %copy.6 = f32[4,32,64,128]{3,2,1,0:T(8,128)} copy(f32[4,32,64,128]{3,2,1,0:T(8,128)} %advect.1) | data formatting | bytes 8388608

commit v2 on v0

v2 whole, which is shorter than its diff:
```python
import functools

import jax
import jax.numpy as jnp
from jax import lax
from jax.experimental import pallas as pl
from jax.experimental.pallas import tpu as pltpu
from jax.sharding import PartitionSpec as P

STEPS = 3
SMOOTH = 0.05
PAD = 8


def kernel(
    sizes, width, lead, den, fj, fi, fk, out, field, flow, k_send, k_recv, k_relay,
    load_sem, south_send, south_recv, east_send, east_recv, down_send, down_recv, relay_send, relay_recv,
):
    _, n_east, n_down = sizes
    nj, ni, nk, ns = den.shape
    chunks = ni // width
    half = n_down // 2
    relays = chunks % half == 0
    rounds = chunks // half
    south, east, down = (lax.axis_index(a) for a in ("south", "east", "down"))
    has_west, has_east = east > 0, east < n_east - 1
    has_up, has_down = down > 0, down < n_down - 1
    inner_k = pl.ds(PAD, nk)
    my_j = jnp.where(south == 0, nj - 1, 0)
    their_j = jnp.where(south == 0, 0, nj + 1)
    rest_j = jnp.where(south == 0, 0, 1)

    def to(axis, index):
        return dict(device_id={axis: index}, device_id_type=pl.DeviceIdType.MESH)

    def each(cond_low, cond_high, fn):
        for side, cond in ((0, cond_low), (1, cond_high)):
            @pl.when(cond)
            def _(side=side):
                fn(side)

    def row_of(c):
        return width * jnp.where(c == 0, 0, jnp.where(c == 1, chunks - 1, c - 1))

    lower = down < half
    at_seam = jnp.logical_or(down == half - 1, down == half)
    mine = lax.rem(down, half)
    own_end = jnp.where(lower, half - 1, half)
    far_end = jnp.where(lower, half, half - 1)
    far_base = jnp.where(lower, half, 0)
    own_base = jnp.where(lower, 0, half)
    own_side = jnp.where(lower, 0, 1)
    is_relay = jnp.logical_not(at_seam)

    barrier = pltpu.get_barrier_semaphore()

    def hello(cond, axis, index):
        @pl.when(cond)
        def _():
            pl.semaphore_signal(barrier, inc=1, **to(axis, index))

    pl.semaphore_signal(barrier, inc=1, **to("south", 1 - south))
    hello(has_west, "east", east - 1)
    hello(has_east, "east", east + 1)
    hello(has_up, "down", down - 1)
    hello(has_down, "down", down + 1)
    targets = 1 + sum(jnp.where(h, 1, 0) for h in (has_west, has_east, has_up, has_down))
    if relays:
        hello(is_relay, "down", own_end)
        for m in range(half):
            hello(jnp.logical_and(at_seam, far_end - far_base != m), "down", far_base + m)
        targets = targets + jnp.where(at_seam, half - 1, 1)

    loads = [
        pltpu.make_async_copy(den.at[my_j], field.at[0, my_j + 1, pl.ds(1, ni), inner_k], load_sem.at[0]),
        pltpu.make_async_copy(
            den.at[pl.ds(rest_j, nj - 1)], field.at[0, pl.ds(rest_j + 1, nj - 1), pl.ds(1, ni), inner_k], load_sem.at[1]),
    ]
    for x, src in enumerate((fj, fi, fk)):
        loads.append(pltpu.make_async_copy(src, flow.at[x], load_sem.at[x + 2]))
    for copy in loads:
        copy.start()

    outside_j = jnp.where(south == 0, 0, nj + 1)

    def clear(n, _):
        for t in range(STEPS):
            field[t, outside_j, n + 1, inner_k] = jnp.zeros((nk, ns), jnp.float32)
        return 0

    lax.fori_loop(0, ni, clear, 0)
    for edge, at in ((jnp.logical_not(has_west), 0), (jnp.logical_not(has_east), ni + 1)):
        @pl.when(edge)
        def _(at=at):
            for t in range(STEPS):
                for j in range(nj):
                    field[t, j + 1, at, inner_k] = jnp.zeros((nk, ns), jnp.float32)
    for edge, side in ((jnp.logical_not(has_up), 0), (jnp.logical_not(has_down), 1)):
        @pl.when(edge)
        def _(side=side):
            for t in range(STEPS):
                for c in range(chunks):
                    k_recv[t, side, c] = jnp.zeros(k_recv.shape[3:], jnp.float32)

    def south_copy(t, c):
        rows = pl.ds(row_of(c) + 1, width)
        return pltpu.make_async_remote_copy(
            src_ref=field.at[t, my_j + 1, rows, inner_k], dst_ref=field.at[t, their_j, rows, inner_k],
            send_sem=south_send.at[t, c], recv_sem=south_recv.at[t, c], **to("south", 1 - south))

    def east_copy(t, side):
        r, dst, other = (1, ni + 1, east - 1) if side == 0 else (ni, 0, east + 1)
        return pltpu.make_async_remote_copy(
            src_ref=field.at[t, pl.ds(1, nj), r, inner_k], dst_ref=field.at[t, pl.ds(1, nj), dst, inner_k],
            send_sem=east_send.at[t, side], recv_sem=east_recv.at[t, 1 - side], **to("east", other))

    def down_copy(t, c, side):
        other = down - 1 if side == 0 else down + 1
        return pltpu.make_async_remote_copy(
            src_ref=k_send.at[t, side, c], dst_ref=k_recv.at[t, 1 - side, c],
            send_sem=down_send.at[t, c, side], recv_sem=down_recv.at[t, c, 1 - side], **to("down", other))

    def detour_copy(t, c, side):
        return pltpu.make_async_remote_copy(
            src_ref=k_send.at[t, side, c], dst_ref=k_relay.at[t, c // half],
            send_sem=down_send.at[t, c, side], recv_sem=relay_recv.at[t, c // half],
            **to("down", own_base + lax.rem(c, half)))

    def hand_on_copy(t, q, side):
        return pltpu.make_async_remote_copy(
            src_ref=k_relay.at[t, q], dst_ref=k_recv.at[t, side, mine + q * half],
            send_sem=relay_send.at[t, q], recv_sem=down_recv.at[t, mine + q * half, side], **to("down", far_end))

    def send_down(t, c):
        def one(side):
            if not relays:
                down_copy(t, c, side).start()
                return
            crosses = down == (half if side == 0 else half - 1)
            around = jnp.logical_and(crosses, own_base + lax.rem(c, half) != own_end)

            @pl.when(around)
            def _():
                detour_copy(t, c, side).start()

            @pl.when(jnp.logical_not(around))
            def _():
                down_copy(t, c, side).start()

        each(has_up, has_down, one)

    def hand_on(t, n):
        if not relays:
            return

        @pl.when(jnp.logical_and(is_relay, lax.rem(n, half) == mine))
        def _():
            q = n // half
            pltpu.make_async_remote_copy(
                src_ref=k_relay.at[t, q], dst_ref=k_relay.at[t, q],
                send_sem=relay_send.at[t, q], recv_sem=relay_recv.at[t, q], **to("down", far_end)).wait_recv()
            hand_on_copy(t, q, own_side).start()

    def ends(t, c, w):
        r = row_of(c) + w + 1
        for j in range(nj):
            yield j + 1, r, pl.ds(w * nj + j, 1)

    def pack(t, c):
        def row(w, _):
            for j, r, at in ends(t, c, w):
                k_send[t, 0, c, at] = field[t, j, r, pl.ds(PAD, 1)]
                k_send[t, 1, c, at] = field[t, j, r, pl.ds(PAD + nk - 1, 1)]
            return 0

        lax.fori_loop(0, width, row, 0)

    def unpack(t, c):
        def row(w, _):
            for j, r, at in ends(t, c, w):
                field[t, j, r, pl.ds(PAD - 1, 1)] = k_recv[t, 0, c, at]
                field[t, j, r, pl.ds(PAD + nk, 1)] = k_recv[t, 1, c, at]
            return 0

        lax.fori_loop(0, width, row, 0)

    def advance(t, c, first, count):
        def row(w, _):
            r = row_of(c) + w
            for b in range(nk // 8):
                at, here = pl.ds(PAD + 8 * b, 8), pl.ds(8 * b, 8)
                column = [field[t, first + p, r + 1, at] for p in range(count + 2)]
                for p in range(count):
                    j = first + p
                    mid, j_low, j_high = column[p + 1], column[p], column[p + 2]
                    i_low, i_high = field[t, j + 1, r, at], field[t, j + 1, r + 2, at]
                    k_low = field[t, j + 1, r + 1, pl.ds(PAD + 8 * b - 1, 8)]
                    k_high = field[t, j + 1, r + 1, pl.ds(PAD + 8 * b + 1, 8)]
                    spread = j_low + j_high + i_low + i_high + k_low + k_high - 6.0 * mid
                    value = (
                        mid - flow[0, j, r, here] * (j_high - j_low) - flow[1, j, r, here] * (i_high - i_low)
                        - flow[2, j, r, here] * (k_high - k_low) + SMOOTH * spread
                    )
                    if t == STEPS - 1:
                        out[j, r, here] = value
                    else:
                        field[t + 1, j + 1, r + 1, at] = value
            return 0

        lax.fori_loop(0, width, row, 0)

    loads[0].wait()
    loads[1].wait()

    def first_pack(c, _):
        pack(0, c)
        return 0

    lax.fori_loop(0, chunks, first_pack, 0)
    pl.semaphore_wait(barrier, targets)

    def first_down(c, _):
        send_down(0, c)
        return 0

    south_copy(0, 0).start()
    lax.fori_loop(0, chunks, first_down, 0)
    each(has_west, has_east, lambda side: east_copy(0, side).start())
    for c in range(1, lead):
        south_copy(0, c).start()
    for copy in loads[2:]:
        copy.wait()

    for t in range(STEPS):
        def chunk(c, _, t=t):
            each(has_up, has_down, lambda side: down_copy(t, c, 1 - side).wait_recv())
            for side, cond in ((0, has_west), (1, has_east)):
                @pl.when(jnp.logical_and(cond, c == side))
                def _(side=side):
                    east_copy(t, 1 - side).wait_recv()

            unpack(t, c)
            advance(t, c, rest_j, nj - 1)

            if t < STEPS - 1:
                @pl.when(c > 0)
                def _():
                    send_down(t + 1, c - 1)

                for side, cond in ((0, has_west), (1, has_east)):
                    @pl.when(jnp.logical_and(cond, c == side + 1))
                    def _(side=side):
                        east_copy(t + 1, side).start()

            if t > 0:
                @pl.when(c == 0)
                def _():
                    send_down(t, chunks - 1)

            late = 2
            if t < STEPS - 1:
                @pl.when(c >= late)
                def _():
                    hand_on(t + 1, c - late)

            if t > 0:
                @pl.when(c < late)
                def _():
                    hand_on(t, c + chunks - late)
            else:
                @pl.when(c == 0)
                def _():
                    for n in range(chunks):
                        hand_on(0, jnp.int32(n))

            south_copy(t, c).wait_recv()

            @pl.when(c + lead < chunks)
            def _():
                south_copy(t, c + lead).start()

            if t < STEPS - 1:
                @pl.when(c + lead >= chunks)
                def _():
                    south_copy(t + 1, c + lead - chunks).start()

            advance(t, c, my_j, 1)
            if t < STEPS - 1:
                pack(t + 1, c)
            return 0

        lax.fori_loop(0, chunks, chunk, 0)

    def finish(c, _):
        for t in range(STEPS):
            south_copy(t, c).wait_send()
            each(has_up, has_down, lambda side: down_copy(t, c, side).wait_send())
        return 0

    lax.fori_loop(0, chunks, finish, 0)
    for t in range(STEPS):
        each(has_west, has_east, lambda side: east_copy(t, side).wait_send())
        if relays:
            @pl.when(is_relay)
            def _():
                for q in range(rounds):
                    hand_on_copy(t, q, 0).wait_send()


def store_kernel(pieces, held, out, sem):
    step = held.shape[0] // pieces
    copies = [
        pltpu.make_async_copy(held.at[pl.ds(p * step, step)], out.at[pl.ds(p * step, step)], sem.at[p])
        for p in range(pieces)
    ]
    for copy in copies:
        copy.start()
    for copy in copies:
        copy.wait()


def solution(mesh, width=8, lead=2):
    sizes = tuple(mesh.shape[a] for a in ("south", "east", "down"))

    def per_device(density, flow_j, flow_i, flow_k):
        nj, ni, nk, ns = density.shape
        chunks = ni // width
        rounds = max(chunks // (sizes[2] // 2), 1)
        dma = pltpu.SemaphoreType.DMA
        held = pl.pallas_call(
            functools.partial(kernel, sizes, width, lead),
            out_shape=pltpu.VMEM(density.shape, density.dtype),
            in_specs=[pl.BlockSpec(memory_space=pl.ANY)] * 4,
            out_specs=pl.BlockSpec(memory_space=pltpu.VMEM),
            scratch_shapes=[
                pltpu.VMEM((STEPS, nj + 2, ni + 2, nk + 2 * PAD, ns), jnp.float32),
                pltpu.VMEM((3, nj, ni, nk, ns), jnp.float32),
                pltpu.VMEM((STEPS, 2, chunks, width * nj, ns), jnp.float32),
                pltpu.VMEM((STEPS, 2, chunks, width * nj, ns), jnp.float32),
                pltpu.VMEM((STEPS, rounds, width * nj, ns), jnp.float32),
                dma((5,)),
                dma((STEPS, chunks)),
                dma((STEPS, chunks)),
                dma((STEPS, 2)),
                dma((STEPS, 2)),
                dma((STEPS, chunks, 2)),
                dma((STEPS, chunks, 2)),
                dma((STEPS, rounds)),
                dma((STEPS, rounds)),
            ],
            compiler_params=pltpu.CompilerParams(
                collective_id=0, has_side_effects=True, vmem_limit_bytes=48 * 1024 * 1024
            ),
            name="advect",
        )(density, flow_j, flow_i, flow_k)
        return pl.pallas_call(
            functools.partial(store_kernel, nj),
            out_shape=jax.ShapeDtypeStruct(density.shape, density.dtype),
            in_specs=[pl.BlockSpec(memory_space=pltpu.VMEM)],
            out_specs=pl.BlockSpec(memory_space=pl.ANY),
            scratch_shapes=[dma((nj,))],
            compiler_params=pltpu.CompilerParams(vmem_limit_bytes=8 * 1024 * 1024),
            name="store",
        )(held)

    spec = P(("ens", "south"), "east", "down", None)
    return jax.shard_map(per_device, mesh=mesh, in_specs=(spec,) * 4, out_specs=spec, check_vma=False)
```

time: 155 us -> 86.3 us (0.56)
  the two profiles are of different devices: /device:TPU:7 before, /device:TPU:1 now
where the time goes in v2:
time: 86.3 us; the launch traced here: 85.5 us
  Pallas kernels  85.5 us (99%)
    pallas_call x1, Pallas kernels, per_device(): pl.pallas_call(functools.partial(kernel, sizes, width, lead), out_shape=p...  83.5 us
    pallas_call x1, Pallas kernels, per_device(): pl.pallas_call(functools.partial(store_kernel, nj), out_shape=jax.ShapeDt...  2.04 us

profile of v2, /device:TPU:1, one launch (start us, length us, event | category | flops | bytes accessed | tf_op | source)
XLA Modules:
  0.0 85.5 jit_solution(7903393071944996426)
XLA Ops:
  0.0 83.5 %advect.1.held = f32[4,32,64,128]{3,2,1,0:T(8,128)S(1)} custom-call(f32[4,32,64,128]{3,2,1,0:T(8,128)} %den.1, f32[4,32,64,128]{3,2,1,0:T(8,128)} %fj.1, f32[4,32,64,128]{3,2,1,0:T(8,128)} %fi.1, f32[4,32,64,128]{3,2,1,0:T(8,128)} %fk.1), custom_call_target="tpu_custom_call" | custom-call | tf_op jit(solution)/shard_map/advect/pallas_call | solution.py:330
  83.5 2.0 %store.1 = f32[4,32,64,128]{3,2,1,0:T(8,128)} custom-call(f32[4,32,64,128]{3,2,1,0:T(8,128)S(1)} %advect.1.held), custom_call_target="tpu_custom_call" | custom-call | tf_op jit(solution)/shard_map/store/pallas_call | solution.py:356

commit v3 on v2

--- a/solution.py
+++ b/solution.py
@@ -14,7 +14,7 @@
 
 def kernel(
     sizes, width, lead, den, fj, fi, fk, out, field, flow, k_send, k_recv, k_relay,
-    load_sem, south_send, south_recv, east_send, east_recv, down_send, down_recv, relay_send, relay_recv,
+    load_sem, south_send, south_recv, east_send, east_recv, down_send, down_recv, relay_send, relay_recv, pair_sem,
 ):
     _, n_east, n_down = sizes
     nj, ni, nk, ns = den.shape
@@ -52,24 +52,31 @@
     own_side = jnp.where(lower, 0, 1)
     is_relay = jnp.logical_not(at_seam)
 
+    even = lax.rem(east, 2) == 0
+    hub = east - lax.rem(east, 2)
     barrier = pltpu.get_barrier_semaphore()
 
-    def hello(cond, axis, index):
+    def hello(cond, index, **others):
         @pl.when(cond)
         def _():
-            pl.semaphore_signal(barrier, inc=1, **to(axis, index))
-
-    pl.semaphore_signal(barrier, inc=1, **to("south", 1 - south))
-    hello(has_west, "east", east - 1)
-    hello(has_east, "east", east + 1)
-    hello(has_up, "down", down - 1)
-    hello(has_down, "down", down + 1)
-    targets = 1 + sum(jnp.where(h, 1, 0) for h in (has_west, has_east, has_up, has_down))
+            pl.semaphore_signal(
+                barrier, inc=1, device_id={"east": index, **others}, device_id_type=pl.DeviceIdType.MESH)
+
+    always = down >= 0
+    near_up = jnp.logical_and(has_up, jnp.logical_not(jnp.logical_and(at_seam, jnp.logical_not(lower))))
+    near_down = jnp.logical_and(has_down, jnp.logical_not(jnp.logical_and(at_seam, lower)))
+    hello(always, hub, south=1 - south)
+    hello(jnp.logical_and(even, has_west), east - 2)
+    hello(jnp.logical_not(even), east - 1)
+    hello(jnp.logical_and(jnp.logical_not(even), has_east), east + 1)
+    hello(near_up, hub, down=down - 1)
+    hello(near_down, hub, down=down + 1)
     if relays:
-        hello(is_relay, "down", own_end)
+        hello(is_relay, hub, down=own_end)
         for m in range(half):
-            hello(jnp.logical_and(at_seam, far_end - far_base != m), "down", far_base + m)
-        targets = targets + jnp.where(at_seam, half - 1, 1)
+            hello(at_seam, hub + 1, down=far_base + m)
+    else:
+        hello(at_seam, hub + 1, down=far_end)
 
     loads = [
         pltpu.make_async_copy(den.at[my_j], field.at[0, my_j + 1, pl.ds(1, ni), inner_k], load_sem.at[0]),
@@ -81,27 +88,6 @@
     for copy in loads:
         copy.start()
 
-    outside_j = jnp.where(south == 0, 0, nj + 1)
-
-    def clear(n, _):
-        for t in range(STEPS):
-            field[t, outside_j, n + 1, inner_k] = jnp.zeros((nk, ns), jnp.float32)
-        return 0
-
-    lax.fori_loop(0, ni, clear, 0)
-    for edge, at in ((jnp.logical_not(has_west), 0), (jnp.logical_not(has_east), ni + 1)):
-        @pl.when(edge)
-        def _(at=at):
-            for t in range(STEPS):
-                for j in range(nj):
-                    field[t, j + 1, at, inner_k] = jnp.zeros((nk, ns), jnp.float32)
-    for edge, side in ((jnp.logical_not(has_up), 0), (jnp.logical_not(has_down), 1)):
-        @pl.when(edge)
-        def _(side=side):
-            for t in range(STEPS):
-                for c in range(chunks):
-                    k_recv[t, side, c] = jnp.zeros(k_recv.shape[3:], jnp.float32)
-
     def south_copy(t, c):
         rows = pl.ds(row_of(c) + 1, width)
         return pltpu.make_async_remote_copy(
@@ -131,19 +117,21 @@
             src_ref=k_relay.at[t, q], dst_ref=k_recv.at[t, side, mine + q * half],
             send_sem=relay_send.at[t, q], recv_sem=down_recv.at[t, mine + q * half, side], **to("down", far_end))
 
-    def send_down(t, c):
+    def send_down(t, c, near=None):
         def one(side):
-            if not relays:
-                down_copy(t, c, side).start()
-                return
             crosses = down == (half if side == 0 else half - 1)
-            around = jnp.logical_and(crosses, own_base + lax.rem(c, half) != own_end)
-
-            @pl.when(around)
-            def _():
-                detour_copy(t, c, side).start()
-
-            @pl.when(jnp.logical_not(around))
+            around = jnp.logical_and(crosses, own_base + lax.rem(c, half) != own_end) if relays else down < 0
+            far = jnp.logical_and(crosses, jnp.logical_not(around))
+            straight = jnp.logical_not(around)
+            if near is not None:
+                straight = far if not near else jnp.logical_not(crosses)
+
+            if near is not False:
+                @pl.when(around)
+                def _():
+                    detour_copy(t, c, side).start()
+
+            @pl.when(straight)
             def _():
                 down_copy(t, c, side).start()
 
@@ -210,107 +198,173 @@
         lax.fori_loop(0, width, row, 0)
 
     loads[0].wait()
+
+    @pl.when(even)
+    def _():
+        one = lambda cond, n: jnp.where(cond, n, 0)
+        pl.semaphore_wait(
+            barrier, 3 + one(east > 0, 1) + one(east < n_east - 2, 1) + one(near_up, 2) + one(near_down, 2)
+            + (one(at_seam, 2 * (half - 1)) if relays else 0))
+        pl.semaphore_signal(pair_sem.at[0], inc=1, **to("east", east + 1))
+
+    @pl.when(jnp.logical_not(even))
+    def _():
+        pl.semaphore_wait(pair_sem.at[0], 1)
+
+    south_copy(0, 0).start()
     loads[1].wait()
+    each(has_west, has_east, lambda side: east_copy(0, side).start())
 
     def first_pack(c, _):
         pack(0, c)
         return 0
 
     lax.fori_loop(0, chunks, first_pack, 0)
-    pl.semaphore_wait(barrier, targets)
 
     def first_down(c, _):
-        send_down(0, c)
+        send_down(0, c, True)
         return 0
 
-    south_copy(0, 0).start()
     lax.fori_loop(0, chunks, first_down, 0)
-    each(has_west, has_east, lambda side: east_copy(0, side).start())
+
+    outside_j = jnp.where(south == 0, 0, nj + 1)
+
+    def clear(n, _):
+        for t in range(STEPS):
+            field[t, outside_j, n + 1, inner_k] = jnp.zeros((nk, ns), jnp.float32)
+        return 0
+
+    lax.fori_loop(0, ni, clear, 0)
+    for edge, at in ((jnp.logical_not(has_west), 0), (jnp.logical_not(has_east), ni + 1)):
+        @pl.when(edge)
+        def _(at=at):
+            for t in range(STEPS):
+                for j in range(nj):
+                    field[t, j + 1, at, inner_k] = jnp.zeros((nk, ns), jnp.float32)
+    for edge, side in ((jnp.logical_not(has_up), 0), (jnp.logical_not(has_down), 1)):
+        @pl.when(edge)
+        def _(side=side):
+            for t in range(STEPS):
+                for c in range(chunks):
+                    k_recv[t, side, c] = jnp.zeros(k_recv.shape[3:], jnp.float32)
+
+    @pl.when(jnp.logical_not(even))
+    def _():
+        pl.semaphore_wait(barrier, 2)
+        pl.semaphore_signal(pair_sem.at[1], inc=1, **to("east", east - 1))
+
+    @pl.when(even)
+    def _():
+        pl.semaphore_wait(pair_sem.at[1], 1)
+
+    def first_far(c, _):
+        send_down(0, c, False)
+        return 0
+
+    lax.fori_loop(0, chunks, first_far, 0)
+    for n in range(chunks):
+        hand_on(0, jnp.int32(n))
     for c in range(1, lead):
         south_copy(0, c).start()
     for copy in loads[2:]:
         copy.wait()
 
-    for t in range(STEPS):
+    def arrive(t, c):
+        south_copy(t, c).wait_recv()
+        if t < STEPS - 1:
+            @pl.when(c > 0)
+            def _():
+                hand_on(t + 1, c - 1)
+
+        if t > 0:
+            @pl.when(c == 0)
+            def _():
+                hand_on(t, c + chunks - 1)
+
+        @pl.when(c + lead < chunks)
+        def _():
+            south_copy(t, c + lead).start()
+
+        if t < STEPS - 1:
+            @pl.when(c + lead >= chunks)
+            def _():
+                south_copy(t + 1, c + lead - chunks).start()
+
+    def surround(t, c):
+        each(has_up, has_down, lambda side: down_copy(t, c, 1 - side).wait_recv())
+        for side, cond in ((0, has_west), (1, has_east)):
+            @pl.when(jnp.logical_and(cond, c == side))
+            def _(side=side):
+                east_copy(t, 1 - side).wait_recv()
+
+        unpack(t, c)
+
+    def sent(t, c):
+        south_copy(t, c).wait_send()
+        each(has_up, has_down, lambda side: down_copy(t, c, side).wait_send())
+
+    for t in range(STEPS - 1):
         def chunk(c, _, t=t):
-            each(has_up, has_down, lambda side: down_copy(t, c, 1 - side).wait_recv())
+            arrive(t, c)
+            surround(t, c)
+            advance(t, c, 0, nj)
+            pack(t + 1, c)
+            send_down(t + 1, c)
             for side, cond in ((0, has_west), (1, has_east)):
                 @pl.when(jnp.logical_and(cond, c == side))
                 def _(side=side):
-                    east_copy(t, 1 - side).wait_recv()
-
-            unpack(t, c)
-            advance(t, c, rest_j, nj - 1)
-
-            if t < STEPS - 1:
-                @pl.when(c > 0)
-                def _():
-                    send_down(t + 1, c - 1)
-
-                for side, cond in ((0, has_west), (1, has_east)):
-                    @pl.when(jnp.logical_and(cond, c == side + 1))
-                    def _(side=side):
-                        east_copy(t + 1, side).start()
-
-            if t > 0:
-                @pl.when(c == 0)
-                def _():
-                    send_down(t, chunks - 1)
-
-            late = 2
-            if t < STEPS - 1:
-                @pl.when(c >= late)
-                def _():
-                    hand_on(t + 1, c - late)
-
-            if t > 0:
-                @pl.when(c < late)
-                def _():
-                    hand_on(t, c + chunks - late)
-            else:
-                @pl.when(c == 0)
-                def _():
-                    for n in range(chunks):
-                        hand_on(0, jnp.int32(n))
-
+                    east_copy(t + 1, side).start()
+            return 0
+
+        lax.fori_loop(0, chunks, chunk, 0)
+
+    t = STEPS - 1
+
+    def last_chunk(c, _):
+        early = c + lead < chunks
+
+        @pl.when(early)
+        def _():
+            arrive(t, c)
+
+        surround(t, c)
+        advance(t, c, rest_j, nj - 1)
+
+        @pl.when(c == chunks - 1)
+        def _():
+            def finish(n, _):
+                for s in range(STEPS - 1):
+                    sent(s, n)
+                each(has_up, has_down, lambda side: down_copy(t, n, side).wait_send())
+                return 0
+
+            lax.fori_loop(0, chunks, finish, 0)
+            for s in range(STEPS):
+                each(has_west, has_east, lambda side: east_copy(s, side).wait_send())
+                if relays:
+                    @pl.when(is_relay)
+                    def _():
+                        for q in range(rounds):
+                            hand_on_copy(s, q, 0).wait_send()
+
+        @pl.when(jnp.logical_not(early))
+        def _():
             south_copy(t, c).wait_recv()
 
-            @pl.when(c + lead < chunks)
-            def _():
-                south_copy(t, c + lead).start()
-
-            if t < STEPS - 1:
-                @pl.when(c + lead >= chunks)
-                def _():
-                    south_copy(t + 1, c + lead - chunks).start()
-
-            advance(t, c, my_j, 1)
-            if t < STEPS - 1:
-                pack(t + 1, c)
-            return 0
-
-        lax.fori_loop(0, chunks, chunk, 0)
-
-    def finish(c, _):
-        for t in range(STEPS):
-            south_copy(t, c).wait_send()
-            each(has_up, has_down, lambda side: down_copy(t, c, side).wait_send())
+        advance(t, c, my_j, 1)
         return 0
 
-    lax.fori_loop(0, chunks, finish, 0)
-    for t in range(STEPS):
-        each(has_west, has_east, lambda side: east_copy(t, side).wait_send())
-        if relays:
-            @pl.when(is_relay)
-            def _():
-                for q in range(rounds):
-                    hand_on_copy(t, q, 0).wait_send()
+    lax.fori_loop(0, chunks, last_chunk, 0)
+    for c in range(chunks):
+        south_copy(t, c).wait_send()
 
 
 def store_kernel(pieces, held, out, sem):
-    step = held.shape[0] // pieces
+    nj, ni = held.shape[:2]
+    step = nj * ni // pieces
     copies = [
-        pltpu.make_async_copy(held.at[pl.ds(p * step, step)], out.at[pl.ds(p * step, step)], sem.at[p])
+        pltpu.make_async_copy(
+            held.at[p * step // ni, pl.ds(p * step % ni, step)], out.at[p * step // ni, pl.ds(p * step % ni, step)], sem.at[p])
         for p in range(pieces)
     ]
     for copy in copies:
@@ -347,6 +401,7 @@
                 dma((STEPS, chunks, 2)),
                 dma((STEPS, rounds)),
                 dma((STEPS, rounds)),
+                pltpu.SemaphoreType.REGULAR((2,)),
             ],
             compiler_params=pltpu.CompilerParams(
                 collective_id=0, has_side_effects=True, vmem_limit_bytes=48 * 1024 * 1024

time: 86.3 us -> 84.6 us (0.980)
  Pallas kernels: 85.5 us -> 84.5 us
    pallas_call x1, Pallas kernels: 83.5 us -> 82.5 us  [per_device(): pl.pallas_call(functools.partial(kernel, sizes, width, lead), out_shape=p...]
where the time goes in v3:
time: 84.6 us; the launch traced here: 84.5 us
  Pallas kernels  84.5 us (100%)
    pallas_call x1, Pallas kernels, per_device(): pl.pallas_call(functools.partial(kernel, sizes, width, lead), out_shape=p...  82.5 us
    pallas_call x1, Pallas kernels, per_device(): pl.pallas_call(functools.partial(store_kernel, nj), out_shape=jax.ShapeDt...  2.04 us

profile of v3, /device:TPU:1, one launch (start us, length us, event | category | flops | bytes accessed | tf_op | source)
XLA Modules:
  0.0 84.5 jit_solution(3996891633327877585)
XLA Ops:
  0.0 82.5 %advect.1.held = f32[4,32,64,128]{3,2,1,0:T(8,128)S(1)} custom-call(f32[4,32,64,128]{3,2,1,0:T(8,128)} %den.1, f32[4,32,64,128]{3,2,1,0:T(8,128)} %fj.1, f32[4,32,64,128]{3,2,1,0:T(8,128)} %fi.1, f32[4,32,64,128]{3,2,1,0:T(8,128)} %fk.1), custom_call_target="tpu_custom_call" | custom-call | tf_op jit(solution)/shard_map/advect/pallas_call | solution.py:384
  82.5 2.0 %store.1 = f32[4,32,64,128]{3,2,1,0:T(8,128)} custom-call(f32[4,32,64,128]{3,2,1,0:T(8,128)S(1)} %advect.1.held), custom_call_target="tpu_custom_call" | custom-call | tf_op jit(solution)/shard_map/store/pallas_call | solution.py:411

commit v4 on v3

--- a/solution.py
+++ b/solution.py
@@ -20,7 +20,7 @@
     nj, ni, nk, ns = den.shape
     chunks = ni // width
     half = n_down // 2
-    relays = chunks % half == 0
+    assert chunks % half == 0
     rounds = chunks // half
     south, east, down = (lax.axis_index(a) for a in ("south", "east", "down"))
     has_west, has_east = east > 0, east < n_east - 1
@@ -52,32 +52,6 @@
     own_side = jnp.where(lower, 0, 1)
     is_relay = jnp.logical_not(at_seam)
 
-    even = lax.rem(east, 2) == 0
-    hub = east - lax.rem(east, 2)
-    barrier = pltpu.get_barrier_semaphore()
-
-    def hello(cond, index, **others):
-        @pl.when(cond)
-        def _():
-            pl.semaphore_signal(
-                barrier, inc=1, device_id={"east": index, **others}, device_id_type=pl.DeviceIdType.MESH)
-
-    always = down >= 0
-    near_up = jnp.logical_and(has_up, jnp.logical_not(jnp.logical_and(at_seam, jnp.logical_not(lower))))
-    near_down = jnp.logical_and(has_down, jnp.logical_not(jnp.logical_and(at_seam, lower)))
-    hello(always, hub, south=1 - south)
-    hello(jnp.logical_and(even, has_west), east - 2)
-    hello(jnp.logical_not(even), east - 1)
-    hello(jnp.logical_and(jnp.logical_not(even), has_east), east + 1)
-    hello(near_up, hub, down=down - 1)
-    hello(near_down, hub, down=down + 1)
-    if relays:
-        hello(is_relay, hub, down=own_end)
-        for m in range(half):
-            hello(at_seam, hub + 1, down=far_base + m)
-    else:
-        hello(at_seam, hub + 1, down=far_end)
-
     loads = [
         pltpu.make_async_copy(den.at[my_j], field.at[0, my_j + 1, pl.ds(1, ni), inner_k], load_sem.at[0]),
         pltpu.make_async_copy(
@@ -85,7 +59,48 @@
     ]
     for x, src in enumerate((fj, fi, fk)):
         loads.append(pltpu.make_async_copy(src, flow.at[x], load_sem.at[x + 2]))
-    for copy in loads:
+    even = lax.rem(east, 2) == 0
+    odd = jnp.logical_not(even)
+    hub = east - lax.rem(east, 2)
+    barrier = pltpu.get_barrier_semaphore()
+
+    def hello(cond, index, **others):
+        @pl.when(cond)
+        def _():
+            pl.semaphore_signal(
+                barrier, inc=1, device_id={"east": index, **others}, device_id_type=pl.DeviceIdType.MESH)
+
+    near_up = jnp.logical_and(has_up, down != half)
+    near_down = jnp.logical_and(has_down, down != half - 1)
+    hello(down >= 0, hub, south=1 - south)
+    hello(odd, hub)
+    loads[0].start()
+    hello(jnp.logical_and(even, has_west), east - 1, south=0)
+    hello(jnp.logical_and(odd, has_east), east + 2, south=0)
+    hello(near_up, hub + 1, south=0, down=down - 1)
+    hello(near_down, hub + 1, south=0, down=down + 1)
+    hello(is_relay, hub + 1, south=0, down=own_end)
+    for m in range(half):
+        hello(at_seam, hub + 1, south=1, down=far_base + m)
+
+    def one(cond, n):
+        return jnp.where(cond, n, 0)
+
+    def learn(n, who, count):
+        taker = jnp.logical_and(odd, south == who)
+
+        @pl.when(taker)
+        def _():
+            pl.semaphore_wait(barrier, count)
+            for s, e in ((who, hub), (1 - who, hub), (1 - who, hub + 1)):
+                pl.semaphore_signal(
+                    pair_sem.at[n], inc=1, device_id={"south": s, "east": e}, device_id_type=pl.DeviceIdType.MESH)
+
+        @pl.when(jnp.logical_not(taker))
+        def _():
+            pl.semaphore_wait(pair_sem.at[n], 1)
+
+    for copy in loads[1:]:
         copy.start()
 
     def south_copy(t, c):
@@ -120,7 +135,7 @@
     def send_down(t, c, near=None):
         def one(side):
             crosses = down == (half if side == 0 else half - 1)
-            around = jnp.logical_and(crosses, own_base + lax.rem(c, half) != own_end) if relays else down < 0
+            around = jnp.logical_and(crosses, own_base + lax.rem(c, half) != own_end)
             far = jnp.logical_and(crosses, jnp.logical_not(around))
             straight = jnp.logical_not(around)
             if near is not None:
@@ -138,9 +153,6 @@
         each(has_up, has_down, one)
 
     def hand_on(t, n):
-        if not relays:
-            return
-
         @pl.when(jnp.logical_and(is_relay, lax.rem(n, half) == mine))
         def _():
             q = n // half
@@ -195,31 +207,30 @@
                         field[t + 1, j + 1, r + 1, at] = value
             return 0
 
-        lax.fori_loop(0, width, row, 0)
+        lax.fori_loop(0, width, row, 0, unroll=2)
 
     loads[0].wait()
 
     @pl.when(even)
     def _():
-        one = lambda cond, n: jnp.where(cond, n, 0)
-        pl.semaphore_wait(
-            barrier, 3 + one(east > 0, 1) + one(east < n_east - 2, 1) + one(near_up, 2) + one(near_down, 2)
-            + (one(at_seam, 2 * (half - 1)) if relays else 0))
+        pl.semaphore_wait(barrier, 3)
         pl.semaphore_signal(pair_sem.at[0], inc=1, **to("east", east + 1))
 
-    @pl.when(jnp.logical_not(even))
+    @pl.when(odd)
     def _():
         pl.semaphore_wait(pair_sem.at[0], 1)
 
     south_copy(0, 0).start()
     loads[1].wait()
-    each(has_west, has_east, lambda side: east_copy(0, side).start())
 
     def first_pack(c, _):
         pack(0, c)
         return 0
 
     lax.fori_loop(0, chunks, first_pack, 0)
+    learn(1, 0, one(hub > 0, 2) + one(hub + 2 < n_east, 2) + one(near_up, 4) + one(near_down, 4)
+          + one(at_seam, 4 * (half - 1)))
+    each(has_west, has_east, lambda side: east_copy(0, side).start())
 
     def first_down(c, _):
         send_down(0, c, True)
@@ -248,14 +259,7 @@
                 for c in range(chunks):
                     k_recv[t, side, c] = jnp.zeros(k_recv.shape[3:], jnp.float32)
 
-    @pl.when(jnp.logical_not(even))
-    def _():
-        pl.semaphore_wait(barrier, 2)
-        pl.semaphore_signal(pair_sem.at[1], inc=1, **to("east", east - 1))
-
-    @pl.when(even)
-    def _():
-        pl.semaphore_wait(pair_sem.at[1], 1)
+    learn(2, 1, 4)
 
     def first_far(c, _):
         send_down(0, c, False)
@@ -269,8 +273,7 @@
     for copy in loads[2:]:
         copy.wait()
 
-    def arrive(t, c):
-        south_copy(t, c).wait_recv()
+    def pass_on(t, c):
         if t < STEPS - 1:
             @pl.when(c > 0)
             def _():
@@ -280,6 +283,10 @@
             @pl.when(c == 0)
             def _():
                 hand_on(t, c + chunks - 1)
+
+    def arrive(t, c):
+        south_copy(t, c).wait_recv()
+        pass_on(t, c)
 
         @pl.when(c + lead < chunks)
         def _():
@@ -341,11 +348,11 @@
             lax.fori_loop(0, chunks, finish, 0)
             for s in range(STEPS):
                 each(has_west, has_east, lambda side: east_copy(s, side).wait_send())
-                if relays:
-                    @pl.when(is_relay)
-                    def _():
-                        for q in range(rounds):
-                            hand_on_copy(s, q, 0).wait_send()
+
+                @pl.when(is_relay)
+                def _(s=s):
+                    for q in range(rounds):
+                        hand_on_copy(s, q, 0).wait_send()
 
         @pl.when(jnp.logical_not(early))
         def _():
@@ -401,7 +408,7 @@
                 dma((STEPS, chunks, 2)),
                 dma((STEPS, rounds)),
                 dma((STEPS, rounds)),
-                pltpu.SemaphoreType.REGULAR((2,)),
+                pltpu.SemaphoreType.REGULAR((3,)),
             ],
             compiler_params=pltpu.CompilerParams(
                 collective_id=0, has_side_effects=True, vmem_limit_bytes=48 * 1024 * 1024

time: 84.6 us -> 82.8 us (0.979)
  Pallas kernels: 84.5 us -> 82.8 us
    pallas_call x1, Pallas kernels: 82.5 us -> 80.7 us  [per_device(): pl.pallas_call(functools.partial(kernel, sizes, width, lead), out_shape=p...]
where the time goes in v4:
time: 82.8 us
  Pallas kernels  82.8 us (100%)
    pallas_call x1, Pallas kernels, per_device(): pl.pallas_call(functools.partial(kernel, sizes, width, lead), out_shape=p...  80.7 us
    pallas_call x1, Pallas kernels, per_device(): pl.pallas_call(functools.partial(store_kernel, nj), out_shape=jax.ShapeDt...  2.04 us

profile of v4, /device:TPU:1, one launch (start us, length us, event | category | flops | bytes accessed | tf_op | source)
XLA Modules:
  0.0 82.8 jit_solution(9463751086011828320)
XLA Ops:
  0.0 80.7 %advect.1.held = f32[4,32,64,128]{3,2,1,0:T(8,128)S(1)} custom-call(f32[4,32,64,128]{3,2,1,0:T(8,128)} %den.1, f32[4,32,64,128]{3,2,1,0:T(8,128)} %fj.1, f32[4,32,64,128]{3,2,1,0:T(8,128)} %fi.1, f32[4,32,64,128]{3,2,1,0:T(8,128)} %fk.1), custom_call_target="tpu_custom_call" | custom-call | tf_op jit(solution)/shard_map/advect/pallas_call | solution.py:391
  80.7 2.0 %store.1 = f32[4,32,64,128]{3,2,1,0:T(8,128)} custom-call(f32[4,32,64,128]{3,2,1,0:T(8,128)S(1)} %advect.1.held), custom_call_target="tpu_custom_call" | custom-call | tf_op jit(solution)/shard_map/store/pallas_call | solution.py:418

commit v5 on v4

--- a/solution.py
+++ b/solution.py
@@ -10,6 +10,7 @@
 STEPS = 3
 SMOOTH = 0.05
 PAD = 8
+ROUTES = ((0, 1, 2, 3), (1, 2, 3, 1), (2, 1, 3, 2))
 
 
 def kernel(
@@ -20,8 +21,7 @@
     nj, ni, nk, ns = den.shape
     chunks = ni // width
     half = n_down // 2
-    assert chunks % half == 0
-    rounds = chunks // half
+    assert chunks == len(ROUTES[0]) == half
     south, east, down = (lax.axis_index(a) for a in ("south", "east", "down"))
     has_west, has_east = east > 0, east < n_east - 1
     has_up, has_down = down > 0, down < n_down - 1
@@ -51,14 +51,26 @@
     own_base = jnp.where(lower, 0, half)
     own_side = jnp.where(lower, 0, 1)
     is_relay = jnp.logical_not(at_seam)
+    def route(t, c):
+        n = ROUTES[t][0]
+        for x in range(1, chunks):
+            n = jnp.where(c == x, ROUTES[t][x], n)
+        return n
+
+
+    def plane_load(n, first, count):
+        return pltpu.make_async_copy(
+            den.at[my_j, pl.ds(first, count)], field.at[0, my_j + 1, pl.ds(first + 1, count), inner_k], load_sem.at[n])
 
     loads = [
-        pltpu.make_async_copy(den.at[my_j], field.at[0, my_j + 1, pl.ds(1, ni), inner_k], load_sem.at[0]),
+        plane_load(0, 0, width),
+        plane_load(1, width, ni - width),
         pltpu.make_async_copy(
-            den.at[pl.ds(rest_j, nj - 1)], field.at[0, pl.ds(rest_j + 1, nj - 1), pl.ds(1, ni), inner_k], load_sem.at[1]),
+            den.at[pl.ds(rest_j, nj - 1)], field.at[0, pl.ds(rest_j + 1, nj - 1), pl.ds(1, ni), inner_k], load_sem.at[2]),
     ]
     for x, src in enumerate((fj, fi, fk)):
-        loads.append(pltpu.make_async_copy(src, flow.at[x], load_sem.at[x + 2]))
+        loads.append(pltpu.make_async_copy(src, flow.at[x], load_sem.at[x + 3]))
+
     even = lax.rem(east, 2) == 0
     odd = jnp.logical_not(even)
     hub = east - lax.rem(east, 2)
@@ -72,9 +84,9 @@
 
     near_up = jnp.logical_and(has_up, down != half)
     near_down = jnp.logical_and(has_down, down != half - 1)
+    loads[0].start()
     hello(down >= 0, hub, south=1 - south)
     hello(odd, hub)
-    loads[0].start()
     hello(jnp.logical_and(even, has_west), east - 1, south=0)
     hello(jnp.logical_and(odd, has_east), east + 2, south=0)
     hello(near_up, hub + 1, south=0, down=down - 1)
@@ -100,11 +112,15 @@
         def _():
             pl.semaphore_wait(pair_sem.at[n], 1)
 
-    for copy in loads[1:]:
+    for copy in loads[1:3]:
         copy.start()
 
-    def south_copy(t, c):
-        rows = pl.ds(row_of(c) + 1, width)
+    def south_copy(t, c, part=None):
+        if part is None:
+            rows = pl.ds(row_of(c) + 1, width)
+        else:
+            rows = pl.ds(row_of(c) + 1 + part * (width // 2), width // 2)
+            c = chunks - 1 + part
         return pltpu.make_async_remote_copy(
             src_ref=field.at[t, my_j + 1, rows, inner_k], dst_ref=field.at[t, their_j, rows, inner_k],
             send_sem=south_send.at[t, c], recv_sem=south_recv.at[t, c], **to("south", 1 - south))
@@ -123,19 +139,19 @@
 
     def detour_copy(t, c, side):
         return pltpu.make_async_remote_copy(
-            src_ref=k_send.at[t, side, c], dst_ref=k_relay.at[t, c // half],
-            send_sem=down_send.at[t, c, side], recv_sem=relay_recv.at[t, c // half],
-            **to("down", own_base + lax.rem(c, half)))
-
-    def hand_on_copy(t, q, side):
+            src_ref=k_send.at[t, side, c], dst_ref=k_relay.at[t, c],
+            send_sem=down_send.at[t, c, side], recv_sem=relay_recv.at[t, c],
+            **to("down", own_base + route(t, c)))
+
+    def hand_on_copy(t, c, side):
         return pltpu.make_async_remote_copy(
-            src_ref=k_relay.at[t, q], dst_ref=k_recv.at[t, side, mine + q * half],
-            send_sem=relay_send.at[t, q], recv_sem=down_recv.at[t, mine + q * half, side], **to("down", far_end))
+            src_ref=k_relay.at[t, c], dst_ref=k_recv.at[t, side, c],
+            send_sem=relay_send.at[t, c], recv_sem=down_recv.at[t, c, side], **to("down", far_end))
 
     def send_down(t, c, near=None):
         def one(side):
             crosses = down == (half if side == 0 else half - 1)
-            around = jnp.logical_and(crosses, own_base + lax.rem(c, half) != own_end)
+            around = jnp.logical_and(crosses, own_base + route(t, c) != own_end)
             far = jnp.logical_and(crosses, jnp.logical_not(around))
             straight = jnp.logical_not(around)
             if near is not None:
@@ -153,13 +169,12 @@
         each(has_up, has_down, one)
 
     def hand_on(t, n):
-        @pl.when(jnp.logical_and(is_relay, lax.rem(n, half) == mine))
-        def _():
-            q = n // half
+        @pl.when(jnp.logical_and(is_relay, route(t, n) == mine))
+        def _():
             pltpu.make_async_remote_copy(
-                src_ref=k_relay.at[t, q], dst_ref=k_relay.at[t, q],
-                send_sem=relay_send.at[t, q], recv_sem=relay_recv.at[t, q], **to("down", far_end)).wait_recv()
-            hand_on_copy(t, q, own_side).start()
+                src_ref=k_relay.at[t, n], dst_ref=k_relay.at[t, n],
+                send_sem=relay_send.at[t, n], recv_sem=relay_recv.at[t, n], **to("down", far_end)).wait_recv()
+            hand_on_copy(t, n, own_side).start()
 
     def ends(t, c, w):
         r = row_of(c) + w + 1
@@ -184,9 +199,9 @@
 
         lax.fori_loop(0, width, row, 0)
 
-    def advance(t, c, first, count):
+    def advance(t, c, first, count, start=0, rows=width):
         def row(w, _):
-            r = row_of(c) + w
+            r = row_of(c) + start + w
             for b in range(nk // 8):
                 at, here = pl.ds(PAD + 8 * b, 8), pl.ds(8 * b, 8)
                 column = [field[t, first + p, r + 1, at] for p in range(count + 2)]
@@ -207,7 +222,7 @@
                         field[t + 1, j + 1, r + 1, at] = value
             return 0
 
-        lax.fori_loop(0, width, row, 0, unroll=2)
+        lax.fori_loop(0, rows, row, 0, unroll=2)
 
     loads[0].wait()
 
@@ -221,7 +236,10 @@
         pl.semaphore_wait(pair_sem.at[0], 1)
 
     south_copy(0, 0).start()
+    for copy in loads[3:]:
+        copy.start()
     loads[1].wait()
+    loads[2].wait()
 
     def first_pack(c, _):
         pack(0, c)
@@ -270,7 +288,7 @@
         hand_on(0, jnp.int32(n))
     for c in range(1, lead):
         south_copy(0, c).start()
-    for copy in loads[2:]:
+    for copy in loads[3:]:
         copy.wait()
 
     def pass_on(t, c):
@@ -288,9 +306,15 @@
         south_copy(t, c).wait_recv()
         pass_on(t, c)
 
-        @pl.when(c + lead < chunks)
+        @pl.when(c + lead < chunks - (1 if t == STEPS - 1 else 0))
         def _():
             south_copy(t, c + lead).start()
+
+        if t == STEPS - 1:
+            @pl.when(c + lead == chunks - 1)
+            def _():
+                for part in (0, 1):
+                    south_copy(t, chunks - 1, part).start()
 
         if t < STEPS - 1:
             @pl.when(c + lead >= chunks)
@@ -348,22 +372,32 @@
             lax.fori_loop(0, chunks, finish, 0)
             for s in range(STEPS):
                 each(has_west, has_east, lambda side: east_copy(s, side).wait_send())
-
-                @pl.when(is_relay)
-                def _(s=s):
-                    for q in range(rounds):
-                        hand_on_copy(s, q, 0).wait_send()
-
-        @pl.when(jnp.logical_not(early))
+                for n in range(chunks):
+                    @pl.when(jnp.logical_and(is_relay, ROUTES[s][n] == mine))
+                    def _(s=s, n=n):
+                        hand_on_copy(s, n, 0).wait_send()
+
+        @pl.when(jnp.logical_not(jnp.logical_or(early, c == chunks - 1)))
         def _():
             south_copy(t, c).wait_recv()
 
-        advance(t, c, my_j, 1)
+        @pl.when(c < chunks - 1)
+        def _():
+            advance(t, c, my_j, 1)
+
+        @pl.when(c == chunks - 1)
+        def _():
+            for part in (0, 1):
+                south_copy(t, chunks - 1, part).wait_recv()
+                advance(t, c, my_j, 1, part * (width // 2), width // 2)
+
         return 0
 
     lax.fori_loop(0, chunks, last_chunk, 0)
-    for c in range(chunks):
+    for c in range(chunks - 1):
         south_copy(t, c).wait_send()
+    for part in (0, 1):
+        south_copy(t, chunks - 1, part).wait_send()
 
 
 def store_kernel(pieces, held, out, sem):
@@ -386,7 +420,6 @@
     def per_device(density, flow_j, flow_i, flow_k):
         nj, ni, nk, ns = density.shape
         chunks = ni // width
-        rounds = max(chunks // (sizes[2] // 2), 1)
         dma = pltpu.SemaphoreType.DMA
         held = pl.pallas_call(
             functools.partial(kernel, sizes, width, lead),
@@ -398,16 +431,16 @@
                 pltpu.VMEM((3, nj, ni, nk, ns), jnp.float32),
                 pltpu.VMEM((STEPS, 2, chunks, width * nj, ns), jnp.float32),
                 pltpu.VMEM((STEPS, 2, chunks, width * nj, ns), jnp.float32),
-                pltpu.VMEM((STEPS, rounds, width * nj, ns), jnp.float32),
-                dma((5,)),
-                dma((STEPS, chunks)),
-                dma((STEPS, chunks)),
+                pltpu.VMEM((STEPS, chunks, width * nj, ns), jnp.float32),
+                dma((6,)),
+                dma((STEPS, chunks + 1)),
+                dma((STEPS, chunks + 1)),
                 dma((STEPS, 2)),
                 dma((STEPS, 2)),
                 dma((STEPS, chunks, 2)),
                 dma((STEPS, chunks, 2)),
-                dma((STEPS, rounds)),
-                dma((STEPS, rounds)),
+                dma((STEPS, chunks)),
+                dma((STEPS, chunks)),
                 pltpu.SemaphoreType.REGULAR((3,)),
             ],
             compiler_params=pltpu.CompilerParams(

time: 82.8 us -> 82 us (level)
  Pallas kernels: 82.8 us -> 81.5 us
    pallas_call x1, Pallas kernels: 80.7 us -> 79.5 us  [per_device(): pl.pallas_call(functools.partial(kernel, sizes, width, lead), out_shape=p...]
where the time goes in v5:
time: 82 us; the launch traced here: 81.5 us
  Pallas kernels  81.5 us (99%)
    pallas_call x1, Pallas kernels, per_device(): pl.pallas_call(functools.partial(kernel, sizes, width, lead), out_shape=p...  79.5 us
    pallas_call x1, Pallas kernels, per_device(): pl.pallas_call(functools.partial(store_kernel, nj), out_shape=jax.ShapeDt...  2.04 us

profile of v5, /device:TPU:1, one launch (start us, length us, event | category | flops | bytes accessed | tf_op | source)
XLA Modules:
  0.0 81.5 jit_solution(3648866538070043938)
XLA Ops:
  0.0 79.5 %advect.1.held = f32[4,32,64,128]{3,2,1,0:T(8,128)S(1)} custom-call(f32[4,32,64,128]{3,2,1,0:T(8,128)} %den.1, f32[4,32,64,128]{3,2,1,0:T(8,128)} %fj.1, f32[4,32,64,128]{3,2,1,0:T(8,128)} %fi.1, f32[4,32,64,128]{3,2,1,0:T(8,128)} %fk.1), custom_call_target="tpu_custom_call" | custom-call | tf_op jit(solution)/shard_map/advect/pallas_call | solution.py:424
  79.5 2.0 %store.1 = f32[4,32,64,128]{3,2,1,0:T(8,128)} custom-call(f32[4,32,64,128]{3,2,1,0:T(8,128)S(1)} %advect.1.held), custom_call_target="tpu_custom_call" | custom-call | tf_op jit(solution)/shard_map/store/pallas_call | solution.py:451

commit v6 on v5

--- a/solution.py
+++ b/solution.py
@@ -73,7 +73,8 @@
 
     even = lax.rem(east, 2) == 0
     odd = jnp.logical_not(even)
-    hub = east - lax.rem(east, 2)
+    base = east - lax.rem(east, 2)
+    hub = base + 1
     barrier = pltpu.get_barrier_semaphore()
 
     def hello(cond, index, **others):
@@ -86,25 +87,25 @@
     near_down = jnp.logical_and(has_down, down != half - 1)
     loads[0].start()
     hello(down >= 0, hub, south=1 - south)
-    hello(odd, hub)
-    hello(jnp.logical_and(even, has_west), east - 1, south=0)
-    hello(jnp.logical_and(odd, has_east), east + 2, south=0)
-    hello(near_up, hub + 1, south=0, down=down - 1)
-    hello(near_down, hub + 1, south=0, down=down + 1)
-    hello(is_relay, hub + 1, south=0, down=own_end)
+    hello(even, hub)
+    hello(jnp.logical_and(even, has_west), east - 2, south=0)
+    hello(jnp.logical_and(odd, has_east), east + 1, south=0)
+    hello(near_up, base, south=0, down=down - 1)
+    hello(near_down, base, south=0, down=down + 1)
+    hello(is_relay, base, south=0, down=own_end)
     for m in range(half):
-        hello(at_seam, hub + 1, south=1, down=far_base + m)
+        hello(at_seam, base, south=1, down=far_base + m)
 
     def one(cond, n):
         return jnp.where(cond, n, 0)
 
     def learn(n, who, count):
-        taker = jnp.logical_and(odd, south == who)
+        taker = jnp.logical_and(even, south == who)
 
         @pl.when(taker)
         def _():
             pl.semaphore_wait(barrier, count)
-            for s, e in ((who, hub), (1 - who, hub), (1 - who, hub + 1)):
+            for s, e in ((who, hub), (1 - who, hub), (1 - who, base)):
                 pl.semaphore_signal(
                     pair_sem.at[n], inc=1, device_id={"south": s, "east": e}, device_id_type=pl.DeviceIdType.MESH)
 
@@ -226,12 +227,12 @@
 
     loads[0].wait()
 
-    @pl.when(even)
+    @pl.when(odd)
     def _():
         pl.semaphore_wait(barrier, 3)
-        pl.semaphore_signal(pair_sem.at[0], inc=1, **to("east", east + 1))
-
-    @pl.when(odd)
+        pl.semaphore_signal(pair_sem.at[0], inc=1, **to("east", east - 1))
+
+    @pl.when(even)
     def _():
         pl.semaphore_wait(pair_sem.at[0], 1)
 
@@ -246,7 +247,7 @@
         return 0
 
     lax.fori_loop(0, chunks, first_pack, 0)
-    learn(1, 0, one(hub > 0, 2) + one(hub + 2 < n_east, 2) + one(near_up, 4) + one(near_down, 4)
+    learn(1, 0, one(base > 0, 2) + one(base + 2 < n_east, 2) + one(near_up, 4) + one(near_down, 4)
           + one(at_seam, 4 * (half - 1)))
     each(has_west, has_east, lambda side: east_copy(0, side).start())
 

time: 82 us -> 81.8 us (level)
  Pallas kernels: 81.5 us -> 80.6 us
    pallas_call x1, Pallas kernels: 79.5 us -> 78.6 us  [per_device(): pl.pallas_call(functools.partial(kernel, sizes, width, lead), out_shape=p...]
where the time goes in v6:
time: 81.8 us; the launch traced here: 80.6 us
  Pallas kernels  80.6 us (99%)
    pallas_call x1, Pallas kernels, per_device(): pl.pallas_call(functools.partial(kernel, sizes, width, lead), out_shape=p...  78.6 us
    pallas_call x1, Pallas kernels, per_device(): pl.pallas_call(functools.partial(store_kernel, nj), out_shape=jax.ShapeDt...  2.04 us

profile of v6, /device:TPU:1, one launch (start us, length us, event | category | flops | bytes accessed | tf_op | source)
XLA Modules:
  0.0 80.6 jit_solution(5328147243175584002)
XLA Ops:
  0.0 78.6 %advect.1.held = f32[4,32,64,128]{3,2,1,0:T(8,128)S(1)} custom-call(f32[4,32,64,128]{3,2,1,0:T(8,128)} %den.1, f32[4,32,64,128]{3,2,1,0:T(8,128)} %fj.1, f32[4,32,64,128]{3,2,1,0:T(8,128)} %fi.1, f32[4,32,64,128]{3,2,1,0:T(8,128)} %fk.1), custom_call_target="tpu_custom_call" | custom-call | tf_op jit(solution)/shard_map/advect/pallas_call | solution.py:425
  78.6 2.0 %store.1 = f32[4,32,64,128]{3,2,1,0:T(8,128)} custom-call(f32[4,32,64,128]{3,2,1,0:T(8,128)S(1)} %advect.1.held), custom_call_target="tpu_custom_call" | custom-call | tf_op jit(solution)/shard_map/store/pallas_call | solution.py:452

commit v7 on v6

--- a/solution.py
+++ b/solution.py
@@ -10,7 +10,7 @@
 STEPS = 3
 SMOOTH = 0.05
 PAD = 8
-ROUTES = ((0, 1, 2, 3), (1, 2, 3, 1), (2, 1, 3, 2))
+ROUTES = ((0, 1, 2, 3), (1, 3, 2, 0), (2, 1, 3, 3))
 
 
 def kernel(

time: 81.8 us -> 81.4 us (level); the launches traced: 80.6 us -> 81.3 us
  no operation moved by 1% of the time
where the time goes in v7:
time: 81.4 us; the launch traced here: 81.3 us
  Pallas kernels  81.3 us (100%)
    pallas_call x1, Pallas kernels, per_device(): pl.pallas_call(functools.partial(kernel, sizes, width, lead), out_shape=p...  79.3 us
    pallas_call x1, Pallas kernels, per_device(): pl.pallas_call(functools.partial(store_kernel, nj), out_shape=jax.ShapeDt...  2.04 us

profile of v7, /device:TPU:1, one launch (start us, length us, event | category | flops | bytes accessed | tf_op | source)
XLA Modules:
  0.0 81.3 jit_solution(17775816543517075249)
XLA Ops:
  0.0 79.3 %advect.1.held = f32[4,32,64,128]{3,2,1,0:T(8,128)S(1)} custom-call(f32[4,32,64,128]{3,2,1,0:T(8,128)} %den.1, f32[4,32,64,128]{3,2,1,0:T(8,128)} %fj.1, f32[4,32,64,128]{3,2,1,0:T(8,128)} %fi.1, f32[4,32,64,128]{3,2,1,0:T(8,128)} %fk.1), custom_call_target="tpu_custom_call" | custom-call | tf_op jit(solution)/shard_map/advect/pallas_call | solution.py:425
  79.3 2.0 %store.1 = f32[4,32,64,128]{3,2,1,0:T(8,128)} custom-call(f32[4,32,64,128]{3,2,1,0:T(8,128)S(1)} %advect.1.held), custom_call_target="tpu_custom_call" | custom-call | tf_op jit(solution)/shard_map/store/pallas_call | solution.py:452

commit v8 on v7

--- a/solution.py
+++ b/solution.py
@@ -9,6 +9,7 @@
 
 STEPS = 3
 SMOOTH = 0.05
+PARTS = 4
 PAD = 8
 ROUTES = ((0, 1, 2, 3), (1, 3, 2, 0), (2, 1, 3, 3))
 
@@ -120,7 +121,7 @@
         if part is None:
             rows = pl.ds(row_of(c) + 1, width)
         else:
-            rows = pl.ds(row_of(c) + 1 + part * (width // 2), width // 2)
+            rows = pl.ds(row_of(c) + 1 + part * (width // PARTS), width // PARTS)
             c = chunks - 1 + part
         return pltpu.make_async_remote_copy(
             src_ref=field.at[t, my_j + 1, rows, inner_k], dst_ref=field.at[t, their_j, rows, inner_k],
@@ -314,7 +315,7 @@
         if t == STEPS - 1:
             @pl.when(c + lead == chunks - 1)
             def _():
-                for part in (0, 1):
+                for part in range(PARTS):
                     south_copy(t, chunks - 1, part).start()
 
         if t < STEPS - 1:
@@ -388,16 +389,16 @@
 
         @pl.when(c == chunks - 1)
         def _():
-            for part in (0, 1):
+            for part in range(PARTS):
                 south_copy(t, chunks - 1, part).wait_recv()
-                advance(t, c, my_j, 1, part * (width // 2), width // 2)
+                advance(t, c, my_j, 1, part * (width // PARTS), width // PARTS)
 
         return 0
 
     lax.fori_loop(0, chunks, last_chunk, 0)
     for c in range(chunks - 1):
         south_copy(t, c).wait_send()
-    for part in (0, 1):
+    for part in range(PARTS):
         south_copy(t, chunks - 1, part).wait_send()
 
 
@@ -434,8 +435,8 @@
                 pltpu.VMEM((STEPS, 2, chunks, width * nj, ns), jnp.float32),
                 pltpu.VMEM((STEPS, chunks, width * nj, ns), jnp.float32),
                 dma((6,)),
-                dma((STEPS, chunks + 1)),
-                dma((STEPS, chunks + 1)),
+                dma((STEPS, chunks + PARTS - 1)),
+                dma((STEPS, chunks + PARTS - 1)),
                 dma((STEPS, 2)),
                 dma((STEPS, 2)),
                 dma((STEPS, chunks, 2)),

time: 81.4 us -> 81.4 us (level)
  no operation moved by 1% of the time
where the time goes in v8:
time: 81.4 us
  Pallas kernels  81.4 us (100%)
    pallas_call x1, Pallas kernels, per_device(): pl.pallas_call(functools.partial(kernel, sizes, width, lead), out_shape=p...  79.3 us
    pallas_call x1, Pallas kernels, per_device(): pl.pallas_call(functools.partial(store_kernel, nj), out_shape=jax.ShapeDt...  2.04 us

profile of v8, /device:TPU:1, one launch (start us, length us, event | category | flops | bytes accessed | tf_op | source)
XLA Modules:
  0.0 81.4 jit_solution(9523330490791663884)
XLA Ops:
  0.0 79.3 %advect.1.held = f32[4,32,64,128]{3,2,1,0:T(8,128)S(1)} custom-call(f32[4,32,64,128]{3,2,1,0:T(8,128)} %den.1, f32[4,32,64,128]{3,2,1,0:T(8,128)} %fj.1, f32[4,32,64,128]{3,2,1,0:T(8,128)} %fi.1, f32[4,32,64,128]{3,2,1,0:T(8,128)} %fk.1), custom_call_target="tpu_custom_call" | custom-call | tf_op jit(solution)/shard_map/advect/pallas_call | solution.py:426
  79.3 2.0 %store.1 = f32[4,32,64,128]{3,2,1,0:T(8,128)} custom-call(f32[4,32,64,128]{3,2,1,0:T(8,128)S(1)} %advect.1.held), custom_call_target="tpu_custom_call" | custom-call | tf_op jit(solution)/shard_map/store/pallas_call | solution.py:453
